TPU v7x, 32 devices: a whole 2x2x4 slice. The times are simulated.
32 devices in a mesh: grp: 2 (over y), row: 4 (over x, core), col: 4 (over z).
Axes of the slice: x: 2, y: 2, z: 4, core: 2. Of those that a mesh axis runs over, the one named last changes fastest.
Arguments:
- sigma_anc: float32 [1536, 768], P(('grp', 'row'), 'col'), parts along dimension 0, may hold values from -3 to 23, as said below
- anc_factor: float32 [1536, 2, 512], P(('grp', 'row', 'col')), parts along dimension 0, may hold values from -0.625 to 0.625
- diag_inverse: float32 [4, 512, 512], P('grp', None, 'row'), parts along dimension 0, may hold values from -0.6 to 1.5, as said below
- pattern: int32 [2, 6], replicated, may hold values from 0 to 1, as said below
Outputs:
- sel_off: float32 [1536, 2, 512], P(('grp', 'row', 'col')), parts along dimension 0
- sel_diag: float32 [4, 512, 512], P('grp'), parts along dimension 0
There are 2 independent parts, one for each index of `grp`. A program takes and returns all parts, laid end to end along the dimension named above; an argument that names none is the same for every part. Nothing has to cross between parts.
Inputs may be any that keep to these rules, and one draw needn't show every extreme that they name: `pattern`: each supernode's present row blocks are a run of consecutive blocks, wrapping around the end, of at least 0 blocks, at most 3, together with some scattered others. `sigma_anc`: symmetric and positive definite. `diag_inverse`: lower triangular, with diagonal entries between 0.5 and 1.5 and small entries below the diagonal.
All inputs are finite; a program needn't handle non-finite values.
Results may differ from a plain program's by a relative error of at most 0.00013.
Values sent between devices are 32-bit elements; how exact they have to be, the bound alone decides.
A program may use at most 64 MiB of HBM per device.

v0:
```python
import functools

import jax
import jax.numpy as jnp
from jax import lax
from jax.experimental import pallas as pl
from jax.experimental.pallas import tpu as pltpu
from jax.sharding import PartitionSpec as P

LANES = 128
SUBLANES = 8


def split(x):
    high = x.astype(jnp.bfloat16)
    low = (x - high.astype(jnp.float32)).astype(jnp.bfloat16)
    return high, low


def dot3(a, b, contract=((1,), (0,))):
    (ah, al), (bh, bl) = a, b
    f = lambda u, v: lax.dot_general(u, v, (contract, ((), ())), preferred_element_type=jnp.float32)
    return f(ah, bh) + (f(ah, bl) + f(al, bh))


def fused_kernel(
    n_r, n_c, supers, width, rows_dev, block_size,
    sig_ref, a_ref, d_ref, pat_ref,
    off_ref, diag_ref,
    ag, sig_t, sq, dfull, pbuf, rbuf, sbuf, rbuf2, left, right, goth, gown, grecv, hx, hrecv, zs, zrecv, res,
    send_sems, s_ag, s_sq, s_d, s_p, s_p2, s_g, s_h, s_z, s_zag, s_xag, s_sib, local_sems,
):
    r = lax.axis_index("row")
    c = lax.axis_index("col")
    n_x = n_r // 2
    x = r // 2
    k = r % 2
    sib = 2 * x + 1 - k
    piece = width // n_r
    nb = width // LANES
    half_rows = nb * (nb + 1) // 2 * LANES
    q = half_rows // (n_x * n_c)
    share = width // (n_r * n_c)
    block_rows = rows_dev * n_c
    sends = []

    def rcopy(src, dst, rsem, row, col):
        cp = pltpu.make_async_remote_copy(
            src_ref=src, dst_ref=dst, send_sem=send_sems.at[len(sends)], recv_sem=rsem,
            device_id={"row": row, "col": col}, device_id_type=pl.DeviceIdType.MESH,
        )
        cp.start()
        sends.append(cp)

    def wait_recv(dst, rsem):
        pltpu.make_async_copy(dst, dst, rsem).wait()

    barrier = pltpu.get_barrier_semaphore()
    sig = lambda row, col: pl.semaphore_signal(
        barrier, inc=1, device_id={"row": row, "col": col}, device_id_type=pl.DeviceIdType.MESH
    )
    for dc in range(1, n_c):
        sig(r, (c + dc) % n_c)
    sig(sib, c)
    for dx in range(1, n_x):
        sig(2 * ((x + dx) % n_x) + k, c)

    pl.semaphore_wait(barrier, n_c + n_x - 1)

    n_line = 70
    part_of = lambda j, h: ag.at[j, :, pl.ds(h * width, width)]
    own_part = lambda h: a_ref.at[:, pl.ds(h * width, width)]

    def line_copy(src, j, d, to, h):
        slot = n_line + (2 * d + (1 if to > 0 else 0)) * supers + h
        return pltpu.make_async_remote_copy(
            src_ref=src, dst_ref=part_of(j, h), send_sem=send_sems.at[slot], recv_sem=s_ag.at[j * supers + h],
            device_id={"row": r, "col": (c + to + n_c) % n_c}, device_id_type=pl.DeviceIdType.MESH,
        )

    def line(d, to, f):
        for cc in range(n_c):
            j = cc - to * d
            if 0 <= j < n_c:
                @pl.when(c == cc)
                def _():
                    f(j, 0 <= cc + to < n_c)

    def start_own(j, onward, to, h):
        if onward:
            line_copy(own_part(h), j, 0, to, h).start()

    for h in range(supers):
        for to in (1, -1):
            line(0, to, functools.partial(start_own, to=to, h=h))
    d_slice = lambda ref, rr: ref.at[:, pl.ds(rr * piece, width - rr * piece), pl.ds(rr * piece, piece)]
    d_src = lambda rr: d_ref.at[:, pl.ds(rr * piece, width - rr * piece), :]

    def d_copy(src, rr, slot, row):
        return pltpu.make_async_remote_copy(
            src_ref=src, dst_ref=d_slice(dfull, rr), send_sem=send_sems.at[slot], recv_sem=s_d.at[rr],
            device_id={"row": row, "col": c}, device_id_type=pl.DeviceIdType.MESH,
        )

    n_fixed = 64
    for rr in range(n_r):
        @pl.when(r == rr)
        def _():
            for dx in range(1, n_x):
                d_copy(d_src(rr), rr, n_fixed + dx, 2 * ((x + dx) % n_x) + k).start()
            d_copy(d_src(rr), rr, n_fixed, sib).start()
            pltpu.make_async_copy(d_src(rr), d_slice(dfull, rr), local_sems.at[0]).start()
    own_copy = pltpu.make_async_copy(a_ref, ag.at[c], local_sems.at[1])
    own_copy.start()

    sig_t[...] = jnp.transpose(sig_ref[...])
    sig_rows = lambda j: pl.ds(pl.multiple_of(j * rows_dev, SUBLANES), rows_dev)
    for dc in range(1, n_c):
        j = (c + dc) % n_c
        rcopy(sig_t.at[sig_rows(j), :], sq.at[c], s_sq.at[c], r, j)
    sq[c] = sig_t[sig_rows(c), :]

    for rr in range(1, n_r):
        dfull[:, 0 : rr * piece, rr * piece : (rr + 1) * piece] = jnp.zeros((supers, rr * piece, piece), jnp.float32)

    def mask_of(first, rows, s):
        row = first + lax.broadcasted_iota(jnp.int32, (rows, 1), 0)
        m = jnp.zeros((rows, 1), jnp.float32)
        for b in range(pat_ref.shape[1]):
            inside = (row >= b * block_size) & (row < (b + 1) * block_size)
            m = jnp.where(inside, pat_ref[s, b].astype(jnp.float32), m)
        return m

    def pass_line(j, onward, to, d, h):
        wait_recv(part_of(j, h), s_ag.at[j * supers + h])
        if onward:
            line_copy(part_of(j, h), j, d, to, h).start()

    for d in range(1, n_c):
        for h in range(supers):
            for to in (1, -1):
                line(d, to, functools.partial(pass_line, to=to, d=d, h=h))

    for rr in range(n_r):
        @pl.when((rr % 2 == k) & (rr // 2 != x))
        def _():
            wait_recv(d_slice(dfull, rr), s_d.at[rr])
            d_copy(d_slice(dfull, rr), rr, n_fixed + n_x + rr // 2, sib).start()

    own_copy.wait()
    for dc in range(1, n_c):
        j = (c + dc) % n_c
        wait_recv(sq.at[j], s_sq.at[j])
    sigma_rows = split(sq[...].reshape(n_r * rows_dev, block_rows))

    for s in range(supers):
        cols = slice(s * width, (s + 1) * width)
        block = ag[:, :, cols].reshape(block_rows, width) * mask_of(r * block_rows, block_rows, s)
        part = dot3(sigma_rows, split(block))
        pbuf[:, :, cols] = part.reshape(n_r, rows_dev, width)
    for i in range(n_x):
        xo = (x + 1 + i) % n_x
        rcopy(pbuf.at[2 * xo + 1 - k], rbuf.at[xo], s_p.at[xo], sib, c)

    for rr in range(n_r):
        @pl.when((rr % 2 != k))
        def _():
            wait_recv(d_slice(dfull, rr), s_d.at[rr])

        @pl.when(r == rr)
        def _():
            pltpu.make_async_copy(d_src(rr), d_slice(dfull, rr), local_sems.at[0]).wait()

    for i in range(n_x):
        xo = (x + 1 + i) % n_x
        wait_recv(rbuf.at[xo], s_p.at[xo])
        sbuf[xo] = pbuf[2 * xo + k] + rbuf[xo]
        if i < n_x - 1:
            rcopy(sbuf.at[xo], rbuf2.at[x], s_p2.at[x], 2 * xo + k, c)

    t_first = (r * n_c + c) * rows_dev
    own_first = (r * n_c + c) * share
    masks = [mask_of(t_first, rows_dev, s) for s in range(supers)]
    step = 2 * LANES

    def times_d(rows_value, s, store):
        for j in range(0, width, step):
            xs = split(rows_value[:, j:])
            ds = split(dfull[s, j:, j : j + step])
            store(j, dot3(xs, ds))

    for s in range(supers):
        def store_scaled(j, v):
            left[s, 0:rows_dev, j : j + step] = -v
        times_d(a_ref[:, s * width : (s + 1) * width] * masks[s], s, store_scaled)
        own = dfull[s, pl.ds(pl.multiple_of(own_first, SUBLANES), share), :]
        left[s, rows_dev:, :] = own
        right[s, rows_dev:, :] = own

    for dx in range(1, n_x):
        xo = (x + dx) % n_x
        wait_recv(rbuf2.at[xo], s_p2.at[xo])
    for s in range(supers):
        cols = slice(s * width, (s + 1) * width)
        y = sbuf[x, :, cols]
        for dx in range(1, n_x):
            y = y + rbuf2[(x + dx) % n_x, :, cols]
        def store_off(j, v):
            right[s, 0:rows_dev, j : j + step] = v
            off_ref[:, s * width + j : s * width + j + step] = v
        times_d(y * (-masks[s]), s, store_off)

    def diag_part(s, dst):
        lh, ll = split(left[s])
        rh, rl = split(right[s])
        b = 0
        for i in range(nb):
            li = slice(i * LANES, (i + 1) * LANES)
            v = dot3((lh[:, li], ll[:, li]), (rh[:, : (i + 1) * LANES], rl[:, : (i + 1) * LANES]), ((0,), (0,)))
            for j in range(i + 1):
                dst[b * LANES : (b + 1) * LANES, :] = v[:, j * LANES : (j + 1) * LANES]
                b += 1

    diag_part(1 - k, goth)
    rcopy(goth, grecv, s_g.at[0], sib, c)

    diag_part(k, gown)
    wait_recv(grecv, s_g.at[0])

    rows_at = lambda xo, j: pl.ds(pl.multiple_of((xo * n_c + j) * q, SUBLANES), q)
    for i in range(n_c):
        j = (c + 1 + i) % n_c
        for dx in range(1, n_x):
            xo = (x + dx) % n_x
            at = rows_at(xo, j)
            hx[at, :] = gown[at, :] + grecv[at, :]
            rcopy(hx.at[at, :], hrecv.at[x, j], s_h.at[x * n_c + j], 2 * xo + k, c)
    for i in range(n_c):
        j = (c + 1 + i) % n_c
        at = rows_at(x, j)
        v = gown[at, :] + grecv[at, :]
        for dx in range(1, n_x):
            xo = (x + dx) % n_x
            wait_recv(hrecv.at[xo, j], s_h.at[xo * n_c + j])
            v = v + hrecv[xo, j]
        zs[j] = v
        if i < n_c - 1:
            rcopy(zs.at[j], zrecv.at[c], s_z.at[c], r, j)

    total = zs[c]
    for dc in range(1, n_c):
        j = (c + dc) % n_c
        wait_recv(zrecv.at[j], s_z.at[j])
        total = total + zrecv[j]
    mine = res.at[k, rows_at(x, c), :]
    res[k, rows_at(x, c), :] = total

    for dc in range(1, n_c):
        rcopy(mine, mine, s_zag.at[c], r, (c + dc) % n_c)
    def pass_on(j):
        chunk = res.at[k, rows_at(x, j), :]
        for dx in range(1, n_x):
            rcopy(chunk, chunk, s_xag.at[x * n_c + j], 2 * ((x + dx) % n_x) + k, c)
        rcopy(chunk, chunk, s_sib.at[x * n_c + j], sib, c)
    pass_on(c)
    for dc in range(1, n_c):
        j = (c + dc) % n_c
        wait_recv(res.at[k, rows_at(x, j), :], s_zag.at[j])
        pass_on(j)
    for dc in range(n_c):
        j = (c + dc) % n_c
        for dx in range(1, n_x):
            xo = (x + dx) % n_x
            chunk = res.at[k, rows_at(xo, j), :]
            wait_recv(chunk, s_xag.at[xo * n_c + j])
            rcopy(chunk, chunk, s_sib.at[xo * n_c + j], sib, c)

    def expand(s):
        b = 0
        for i in range(nb):
            for j in range(i + 1):
                v = res[s, b * LANES : (b + 1) * LANES, :]
                diag_ref[s, i * LANES : (i + 1) * LANES, j * LANES : (j + 1) * LANES] = v
                if j < i:
                    diag_ref[s, j * LANES : (j + 1) * LANES, i * LANES : (i + 1) * LANES] = jnp.transpose(v)
                b += 1

    expand(k)
    for xo in range(n_x):
        for j in range(n_c):
            wait_recv(res.at[1 - k, rows_at(xo, j), :], s_sib.at[xo * n_c + j])
    expand(1 - k)

    for cp in sends:
        cp.wait_send()
    for rr in range(n_r):
        @pl.when(r == rr)
        def _():
            for dx in range(1, n_x):
                d_copy(d_src(rr), rr, n_fixed + dx, 2 * ((x + dx) % n_x) + k).wait_send()
            d_copy(d_src(rr), rr, n_fixed, sib).wait_send()

        @pl.when((rr % 2 == k) & (rr // 2 != x))
        def _():
            d_copy(d_slice(dfull, rr), rr, n_fixed + n_x + rr // 2, sib).wait_send()

    def sent(j, onward, to, d, h):
        if onward:
            line_copy(own_part(h), j, d, to, h).wait_send()

    for d in range(n_c):
        for h in range(supers):
            for to in (1, -1):
                line(d, to, functools.partial(sent, to=to, d=d, h=h))


def fused_body(sigma_anc, anc_factor, diag_inverse, pattern):
    rows_dev, supers, width = anc_factor.shape
    n_r = lax.axis_size("row")
    n_c = lax.axis_size("col")
    n_x = n_r // 2
    total_rows = rows_dev * n_r * n_c
    flat = supers * width
    nb = width // LANES
    half_rows = nb * (nb + 1) // 2 * LANES
    q = half_rows // (n_x * n_c)
    share = width // (n_r * n_c)
    f32 = lambda *shape: pltpu.VMEM(shape, jnp.float32)
    dma = lambda n: pltpu.SemaphoreType.DMA((n,))
    vm = pl.BlockSpec(memory_space=pltpu.VMEM)
    off, diag = pl.pallas_call(
        functools.partial(fused_kernel, n_r, n_c, supers, width, rows_dev, total_rows // pattern.shape[1]),
        out_shape=(
            jax.ShapeDtypeStruct((rows_dev, flat), jnp.float32),
            jax.ShapeDtypeStruct((supers, width, width), jnp.float32),
        ),
        in_specs=[vm, vm, vm, pl.BlockSpec(memory_space=pltpu.SMEM)],
        out_specs=(vm, vm),
        scratch_shapes=[
            f32(n_c, rows_dev, flat),
            f32(n_r * rows_dev, n_c * rows_dev),
            f32(n_c, rows_dev, n_c * rows_dev),
            f32(supers, width, width),
            f32(n_r, rows_dev, flat),
            f32(n_x, rows_dev, flat),
            f32(n_x, rows_dev, flat),
            f32(n_x, rows_dev, flat),
            f32(supers, rows_dev + share, width),
            f32(supers, rows_dev + share, width),
            f32(half_rows, LANES),
            f32(half_rows, LANES),
            f32(half_rows, LANES),
            f32(half_rows, LANES),
            f32(n_x, n_c, q, LANES),
            f32(n_c, q, LANES),
            f32(n_c, q, LANES),
            f32(supers, half_rows, LANES),
            dma(70 + 2 * n_c * supers),
            dma(n_c * supers), dma(n_c), dma(n_r), dma(n_x), dma(n_x), dma(1), dma(n_x * n_c), dma(n_c), dma(n_c),
            dma(n_x * n_c), dma(n_x * n_c), dma(2),
        ],
        compiler_params=pltpu.CompilerParams(
            collective_id=0, has_side_effects=True, vmem_limit_bytes=56 * 1024 * 1024
        ),
    )(sigma_anc, anc_factor.reshape(rows_dev, flat), diag_inverse, pattern)
    return off.reshape(anc_factor.shape), diag


def fits(sigma_anc, anc_factor, diag_inverse):
    rows_dev, supers, width = anc_factor.shape
    n_r = lax.axis_size("row")
    n_c = lax.axis_size("col")
    nb = width // LANES
    chunks = (n_r // 2) * n_c * SUBLANES
    return (
        n_r == n_c
        and n_r % 2 == 0
        and supers == 2
        and sigma_anc.shape[0] == sigma_anc.shape[1]
        and diag_inverse.shape[2] % LANES == 0
        and width % (2 * LANES) == 0
        and rows_dev % SUBLANES == 0
        and width % (n_r * n_c * SUBLANES) == 0
        and (nb * (nb + 1) // 2 * LANES) % chunks == 0
    )


def plain_body(sigma_anc, anc_factor, diag_inverse, pattern):
    precise = lax.Precision.HIGHEST
    rows_dev, supers, super_width = anc_factor.shape
    row_count = lax.axis_size("row")
    col_count = lax.axis_size("col")
    position = lax.axis_index("row") * col_count + lax.axis_index("col")
    total_rows = rows_dev * row_count * col_count
    block_size = total_rows // pattern.shape[1]
    flat_mask = jnp.repeat(pattern.astype(jnp.float32), block_size, axis=1)
    own_mask = jnp.transpose(lax.dynamic_slice_in_dim(flat_mask, position * rows_dev, rows_dev, 1))[
        :, :, None
    ]
    device_total = row_count * col_count
    share = -(-super_width // device_total)
    masked_factor = anc_factor * own_mask
    flattened = masked_factor.reshape(rows_dev, -1)
    gathered = lax.all_gather(flattened, "row", axis=0, tiled=True)
    stacked = gathered.reshape(row_count, rows_dev, flattened.shape[1])
    turned = lax.all_to_all(stacked, "col", split_axis=0, concat_axis=1, tiled=True)
    column_block = turned.reshape(row_count * rows_dev, flattened.shape[1])
    summed_rows = lax.psum_scatter(
        jnp.dot(sigma_anc, column_block, precision=precise, preferred_element_type=jnp.float32),
        "col",
        scatter_dimension=0,
        tiled=True,
    )
    off_factor = -(summed_rows.reshape(masked_factor.shape) * own_mask)
    both_rows = jnp.concatenate([masked_factor, off_factor], axis=0)
    column_piece = lax.all_gather(diag_inverse, "row", axis=2, tiled=True)
    product = jnp.einsum("rsk,skj->rsj", both_rows, column_piece, precision=precise)
    own_rows = lax.dynamic_slice_in_dim(column_piece, position * share, share, 1)
    scaled = product[:rows_dev]
    sel_off = product[rows_dev:]
    diag_term = jnp.einsum("skj,skl->sjl", own_rows, own_rows, precision=precise)
    partial_value = diag_term - jnp.einsum("rsj,rsl->sjl", scaled, sel_off, precision=precise)
    sel_diag = lax.psum(partial_value, ("row", "col"))
    return (sel_off, sel_diag)


def body(sigma_anc, anc_factor, diag_inverse, pattern):
    run = fused_body if fits(sigma_anc, anc_factor, diag_inverse) else plain_body
    return run(sigma_anc, anc_factor, diag_inverse, pattern)


def solution(mesh):
    return jax.shard_map(
        body,
        mesh=mesh,
        in_specs=(
            P(("grp", "row"), "col"),
            P(("grp", "row", "col"), None, None),
            P("grp", None, "row"),
            P(),
        ),
        out_specs=(P(("grp", "row", "col"), None, None), P("grp", None, None)),
        check_vma=False,
    )
```

profile of v0, /device:TPU:9, one launch (start us, length us, event | category | flops | bytes accessed | tf_op | source)
XLA Modules:
  0.0 68.8 jit_solution(18198193782254563526)
XLA Ops:
  0.6 1.6 %copy.6 = f32[6,8,2,512]{3,1,2,0:T(8,128)} copy(f32[6,8,2,512]{3,2,1,0:T(2,128)} %bitcast.3) | data formatting | bytes 393216
  2.3 61.7 %shard_map.59 = (f32[48,1024]{1,0:T(8,128)}, f32[2,512,512]{2,1,0:T(8,128)}) custom-call(f32[192,192]{1,0:T(8,128)} %sig_ref.1, f32[48,1024]{1,0:T(8,128)} %bitcast.2, f32[2,512,128]{2,1,0:T(8,128)} %d_ref.1, s32[2,6]{1,0:T(2,128)} %pat_ref.1), custom_call_target="tpu_custom_call" | custom-call | tf_op jit(solution)/shard_map/pallas_call | solution.py:331
  64.0 1.8 %reshape.11 = f32[48,2,512]{2,1,0:T(2,128)} reshape(f32[48,1024]{1,0:T(8,128)} %get-tuple-element.4) | data formatting | bytes 393216 | tf_op jit(solution)/shard_map/reshape | solution.py:366
  65.8 3.1 %copy.8 = f32[2,512,512]{2,1,0:T(8,128)} copy(f32[2,512,512]{2,1,0:T(8,128)} %get-tuple-element.9) | data formatting | bytes 4194304
where the time goes:
time: 69.1 us; the launch traced here: 68.8 us
  Pallas kernels  61.7 us (89%)
  local copies, waits for them, and re-layouts  6.48 us (9%)
    pallas_call x1, Pallas kernels, fused_body(): pl.pallas_call(functools.partial(fused_kernel, n_r, n_c, supers, width, r...  61.7 us
    unnamed x2, local copies, waits for them, and re-layouts  4.72 us
    reshape x1, local copies, waits for them, and re-layouts, fused_body(): return (off.reshape(anc_factor.shape), diag)  1.76 us

commit v1 on v0

--- a/solution.py
+++ b/solution.py
@@ -26,8 +26,8 @@
 def fused_kernel(
     n_r, n_c, supers, width, rows_dev, block_size,
     sig_ref, a_ref, d_ref, pat_ref,
-    off_ref, diag_ref,
-    ag, sig_t, sq, dfull, pbuf, rbuf, sbuf, rbuf2, left, right, goth, gown, grecv, hx, hrecv, zs, zrecv, res,
+    off_ref, res,
+    av, ag, sig_t, sq, dfull, pbuf, rbuf, sbuf, rbuf2, left, right, goth, gown, grecv, hx, hrecv, zs, zrecv,
     send_sems, s_ag, s_sq, s_d, s_p, s_p2, s_g, s_h, s_z, s_zag, s_xag, s_sib, local_sems,
 ):
     r = lax.axis_index("row")
@@ -67,9 +67,14 @@
 
     pl.semaphore_wait(barrier, n_c + n_x - 1)
 
+    for h in range(supers):
+        for t in range(nb):
+            rows = a_ref[pl.ds(t * supers + h, rows_dev, stride=nb * supers), :]
+            av[:, h * width + t * LANES : h * width + (t + 1) * LANES] = rows
+
     n_line = 70
     part_of = lambda j, h: ag.at[j, :, pl.ds(h * width, width)]
-    own_part = lambda h: a_ref.at[:, pl.ds(h * width, width)]
+    own_part = lambda h: av.at[:, pl.ds(h * width, width)]
 
     def line_copy(src, j, d, to, h):
         slot = n_line + (2 * d + (1 if to > 0 else 0)) * supers + h
@@ -110,7 +115,7 @@
                 d_copy(d_src(rr), rr, n_fixed + dx, 2 * ((x + dx) % n_x) + k).start()
             d_copy(d_src(rr), rr, n_fixed, sib).start()
             pltpu.make_async_copy(d_src(rr), d_slice(dfull, rr), local_sems.at[0]).start()
-    own_copy = pltpu.make_async_copy(a_ref, ag.at[c], local_sems.at[1])
+    own_copy = pltpu.make_async_copy(av, ag.at[c], local_sems.at[1])
     own_copy.start()
 
     sig_t[...] = jnp.transpose(sig_ref[...])
@@ -192,7 +197,7 @@
     for s in range(supers):
         def store_scaled(j, v):
             left[s, 0:rows_dev, j : j + step] = -v
-        times_d(a_ref[:, s * width : (s + 1) * width] * masks[s], s, store_scaled)
+        times_d(av[:, s * width : (s + 1) * width] * masks[s], s, store_scaled)
         own = dfull[s, pl.ds(pl.multiple_of(own_first, SUBLANES), share), :]
         left[s, rows_dev:, :] = own
         right[s, rows_dev:, :] = own
@@ -207,7 +212,9 @@
             y = y + rbuf2[(x + dx) % n_x, :, cols]
         def store_off(j, v):
             right[s, 0:rows_dev, j : j + step] = v
-            off_ref[:, s * width + j : s * width + j + step] = v
+            for t in range(j // LANES, (j + step) // LANES):
+                at = pl.ds(t * supers + s, rows_dev, stride=nb * supers)
+                off_ref[at, :] = v[:, t * LANES - j : (t + 1) * LANES - j]
         times_d(y * (-masks[s]), s, store_off)
 
     def diag_part(s, dst):
@@ -275,21 +282,9 @@
             wait_recv(chunk, s_xag.at[xo * n_c + j])
             rcopy(chunk, chunk, s_sib.at[xo * n_c + j], sib, c)
 
-    def expand(s):
-        b = 0
-        for i in range(nb):
-            for j in range(i + 1):
-                v = res[s, b * LANES : (b + 1) * LANES, :]
-                diag_ref[s, i * LANES : (i + 1) * LANES, j * LANES : (j + 1) * LANES] = v
-                if j < i:
-                    diag_ref[s, j * LANES : (j + 1) * LANES, i * LANES : (i + 1) * LANES] = jnp.transpose(v)
-                b += 1
-
-    expand(k)
     for xo in range(n_x):
         for j in range(n_c):
             wait_recv(res.at[1 - k, rows_at(xo, j), :], s_sib.at[xo * n_c + j])
-    expand(1 - k)
 
     for cp in sends:
         cp.wait_send()
@@ -312,6 +307,23 @@
         for h in range(supers):
             for to in (1, -1):
                 line(d, to, functools.partial(sent, to=to, d=d, h=h))
+
+
+def unpack_kernel(supers, nb, off_in, res, off_out, diag_out, stage, sems):
+    copies = [pltpu.make_async_copy(off_in, off_out, sems.at[supers * nb])]
+    copies[0].start()
+    for s in range(supers):
+        for i in range(nb):
+            for j in range(nb):
+                hi, lo = max(i, j), min(i, j)
+                b = hi * (hi + 1) // 2 + lo
+                v = res[s, b * LANES : (b + 1) * LANES, :]
+                stage[s, i * LANES : (i + 1) * LANES, j * LANES : (j + 1) * LANES] = v if i >= j else jnp.transpose(v)
+            at = (s, pl.ds(i * LANES, LANES))
+            copies.append(pltpu.make_async_copy(stage.at[at], diag_out.at[at], sems.at[s * nb + i]))
+            copies[-1].start()
+    for cp in copies:
+        cp.wait()
 
 
 def fused_body(sigma_anc, anc_factor, diag_inverse, pattern):
@@ -328,15 +340,18 @@
     f32 = lambda *shape: pltpu.VMEM(shape, jnp.float32)
     dma = lambda n: pltpu.SemaphoreType.DMA((n,))
     vm = pl.BlockSpec(memory_space=pltpu.VMEM)
-    off, diag = pl.pallas_call(
+    linear = jnp.transpose(anc_factor.reshape(rows_dev, supers, nb, LANES), (0, 2, 1, 3))
+    linear = linear.reshape(rows_dev * nb * supers, LANES)
+    off, res = pl.pallas_call(
         functools.partial(fused_kernel, n_r, n_c, supers, width, rows_dev, total_rows // pattern.shape[1]),
         out_shape=(
-            jax.ShapeDtypeStruct((rows_dev, flat), jnp.float32),
-            jax.ShapeDtypeStruct((supers, width, width), jnp.float32),
+            pltpu.VMEM((rows_dev * supers * nb, LANES), jnp.float32),
+            pltpu.VMEM((supers, half_rows, LANES), jnp.float32),
         ),
         in_specs=[vm, vm, vm, pl.BlockSpec(memory_space=pltpu.SMEM)],
         out_specs=(vm, vm),
         scratch_shapes=[
+            f32(rows_dev, flat),
             f32(n_c, rows_dev, flat),
             f32(n_r * rows_dev, n_c * rows_dev),
             f32(n_c, rows_dev, n_c * rows_dev),
@@ -354,7 +369,6 @@
             f32(n_x, n_c, q, LANES),
             f32(n_c, q, LANES),
             f32(n_c, q, LANES),
-            f32(supers, half_rows, LANES),
             dma(70 + 2 * n_c * supers),
             dma(n_c * supers), dma(n_c), dma(n_r), dma(n_x), dma(n_x), dma(1), dma(n_x * n_c), dma(n_c), dma(n_c),
             dma(n_x * n_c), dma(n_x * n_c), dma(2),
@@ -362,7 +376,20 @@
         compiler_params=pltpu.CompilerParams(
             collective_id=0, has_side_effects=True, vmem_limit_bytes=56 * 1024 * 1024
         ),
-    )(sigma_anc, anc_factor.reshape(rows_dev, flat), diag_inverse, pattern)
+    )(sigma_anc, linear, diag_inverse, pattern)
+    hbm = pl.BlockSpec(memory_space=pl.ANY)
+    off, diag = pl.pallas_call(
+        functools.partial(unpack_kernel, supers, nb),
+        out_shape=(
+            jax.ShapeDtypeStruct(off.shape, jnp.float32),
+            jax.ShapeDtypeStruct((supers, width, width), jnp.float32),
+        ),
+        in_specs=[vm, vm],
+        out_specs=(hbm, hbm),
+        scratch_shapes=[f32(supers, width, width), dma(supers * nb + 1)],
+        compiler_params=pltpu.CompilerParams(vmem_limit_bytes=8 * 1024 * 1024),
+    )(off, res)
+    off = jnp.transpose(off.reshape(rows_dev, nb, supers, LANES), (0, 2, 1, 3))
     return off.reshape(anc_factor.shape), diag
 
 

time: 69.1 us -> 62.6 us (0.906)
  the two profiles are of different devices: /device:TPU:9 before, /device:TPU:13 now
where the time goes in v1:
time: 62.6 us; the launch traced here: 62.4 us
  Pallas kernels  61.8 us (99%)
  between operations  0.64 us (1%)
    pallas_call x1, Pallas kernels, fused_body(): pl.pallas_call(functools.partial(fused_kernel, n_r, n_c, supers, width, r...  60.2 us
    pallas_call x1, Pallas kernels, fused_body(): pl.pallas_call(functools.partial(unpack_kernel, supers, nb), out_shape=(j...  1.52 us

profile of v1, /device:TPU:13, one launch (start us, length us, event | category | flops | bytes accessed | tf_op | source)
XLA Modules:
  0.0 62.4 jit_solution(17781842820126427353)
XLA Ops:
  0.6 60.2 %shard_map.59 = (f32[384,128]{1,0:T(8,128)S(1)}, f32[2,1280,128]{2,1,0:T(8,128)S(1)}) custom-call(f32[192,192]{1,0:T(8,128)} %sig_ref.1, f32[384,128]{1,0:T(8,128)} %bitcast.10, f32[2,512,128]{2,1,0:T(8,128)} %d_ref.1, s32[2,6]{1,0:T(2,128)} %pat_ref.1), custom_call_target="tpu_custom_call" | custom-call | tf_op jit(solution)/shard_map/pallas_call | solution.py:345
  60.9 1.5 %shard_map.60 = (f32[384,128]{1,0:T(8,128)}, f32[2,512,512]{2,1,0:T(8,128)}) custom-call(f32[384,128]{1,0:T(8,128)S(1)} %get-tuple-element.6.off_in, f32[2,1280,128]{2,1,0:T(8,128)S(1)} %get-tuple-element.7.res), custom_call_target="tpu_custom_call" | custom-call | tf_op jit(solution)/shard_map/pallas_call | solution.py:381

commit v2 on v1

v2 whole, which is shorter than its diff:
```python
import functools

import jax
import jax.numpy as jnp
from jax import lax
from jax.experimental import pallas as pl
from jax.experimental.pallas import tpu as pltpu
from jax.sharding import PartitionSpec as P

LANES = 128
SUBLANES = 8


def split(x):
    high = x.astype(jnp.bfloat16)
    low = (x - high.astype(jnp.float32)).astype(jnp.bfloat16)
    return high, low


def dot3(a, b, contract=((1,), (0,))):
    (ah, al), (bh, bl) = a, b
    f = lambda u, v: lax.dot_general(u, v, (contract, ((), ())), preferred_element_type=jnp.float32)
    return f(ah, bh) + (f(ah, bl) + f(al, bh))


def columns_of(nb):
    return [[j for j in range(nb) if (j + j // 2) % 2 == core] for core in range(2)]


def pairs_of(nb):
    columns = columns_of(nb)
    pairs = [[], []]
    every = [(i, j) for i in range(nb) for j in range(i + 1)]
    owners = lambda pair: [core for core in range(2) if pair[0] in columns[core] or pair[1] in columns[core]]
    for pair in sorted(every, key=lambda p: len(owners(p))):
        pairs[min(owners(pair), key=lambda core: len(pairs[core]))].append(pair)
    return pairs


def fused_kernel(
    n_r, n_c, supers, width, rows_dev, block_size,
    sig_ref, a_ref, d_ref, pat_ref,
    off_ref, res,
    av, sig_t, wz, sq, dfull, scl, vpart, vrecv, of, offr, gpart, hrecv,
    send_sems, s_w, s_sq, s_sx, s_d, s_scl, s_v, s_off, s_h, s_zag, s_xag, s_sib, local_sems,
):
    r = lax.axis_index("row")
    c = lax.axis_index("col")
    x = r // 2
    k = r % 2
    sib = 2 * x + 1 - k
    par = 2 * (1 - x) + k
    dia = 2 * (1 - x) + 1 - k
    piece = width // n_r
    nb = width // LANES
    half = width // 2
    share = width // n_c
    block_rows = rows_dev * n_c
    columns = columns_of(nb)
    pairs = pairs_of(nb)
    q = len(pairs[0]) * LANES // n_c
    sends = []

    def copy_to(src, dst, rsem, row, col, slot):
        return pltpu.make_async_remote_copy(
            src_ref=src, dst_ref=dst, send_sem=send_sems.at[slot], recv_sem=rsem,
            device_id={"row": row, "col": col}, device_id_type=pl.DeviceIdType.MESH,
        )

    first_slot = 4

    def rcopy(src, dst, rsem, row, col):
        cp = copy_to(src, dst, rsem, row, col, first_slot + len(sends))
        cp.start()
        sends.append(cp)

    def wait_recv(dst, rsem):
        pltpu.make_async_copy(dst, dst, rsem).wait()

    others = [(c + dc) % n_c for dc in range(1, n_c)]
    barrier = pltpu.get_barrier_semaphore()
    sig = lambda row, col: pl.semaphore_signal(
        barrier, inc=1, device_id={"row": row, "col": col}, device_id_type=pl.DeviceIdType.MESH
    )
    for j in others:
        sig(r, j)
    for row in (sib, par, dia):
        sig(row, c)

    def mask_of(first, rows, s):
        row = first + lax.broadcasted_iota(jnp.int32, (rows, 1), 0)
        m = jnp.zeros((rows, 1), jnp.float32)
        for b in range(pat_ref.shape[1]):
            inside = (row >= b * block_size) & (row < (b + 1) * block_size)
            m = jnp.where(inside, pat_ref[s, b].astype(jnp.float32), m)
        return m

    for s in range(supers):
        mask = mask_of((r * n_c + c) * rows_dev, rows_dev, s)
        for t in range(nb):
            rows = a_ref[pl.ds(t * supers + s, rows_dev, stride=nb * supers), :]
            av[s, :, t * LANES : (t + 1) * LANES] = rows * mask
    sig_t[...] = jnp.transpose(sig_ref[...])

    pl.semaphore_wait(barrier, n_c + 2)

    sig_rows = lambda j: pl.ds(pl.multiple_of(j * rows_dev, SUBLANES), rows_dev)
    rcopy(av.at[1 - x], wz.at[1, c], s_w.at[n_c + c], par, c)
    for j in others:
        rcopy(sig_t.at[sig_rows(j), :], sq.at[0, c], s_sq.at[c], r, j)
    for j in others:
        rcopy(av.at[x], wz.at[0, c], s_w.at[c], r, j)
    own_copy = pltpu.make_async_copy(av.at[x], wz.at[0, c], local_sems.at[1])
    own_copy.start()

    d_slice = lambda rr: dfull.at[pl.ds(rr * piece, width - rr * piece), pl.ds(rr * piece, piece)]
    d_src = lambda rr, s: d_ref.at[s, pl.ds(rr * piece, width - rr * piece), :]
    for rr in range(n_r):
        @pl.when(r == rr)
        def _():
            copy_to(d_src(rr, 1 - x), d_slice(rr), s_d.at[rr], par, c, 0).start()
            copy_to(d_src(rr, x), d_slice(rr), s_d.at[rr], sib, c, 1).start()
            pltpu.make_async_copy(d_src(rr, x), d_slice(rr), local_sems.at[0]).start()

    sq[0, c] = sig_t[sig_rows(c), :]
    for rr in range(1, n_r):
        dfull[0 : rr * piece, rr * piece : (rr + 1) * piece] = jnp.zeros((rr * piece, piece), jnp.float32)

    wait_recv(wz.at[1, c], s_w.at[n_c + c])
    for j in others:
        rcopy(wz.at[1, c], wz.at[1, c], s_w.at[n_c + c], r, j)
    for j in others:
        wait_recv(sq.at[0, j], s_sq.at[j])
    rcopy(sq.at[0], sq.at[1], s_sx.at[0], par, c)

    for rr in range(n_r):
        @pl.when(rr == par)
        def _():
            wait_recv(d_slice(rr), s_d.at[rr])
            copy_to(d_slice(rr), d_slice(rr), s_d.at[rr], sib, c, 2).start()
    for rr in range(n_r):
        @pl.when((rr == sib) | (rr == dia))
        def _():
            wait_recv(d_slice(rr), s_d.at[rr])

        @pl.when(rr == r)
        def _():
            pltpu.make_async_copy(d_src(rr, x), d_slice(rr), local_sems.at[0]).wait()

    own_copy.wait()
    near = split(jnp.concatenate([wz[0, c], wz[1, c]], axis=0))
    for j in range(0, width, LANES):
        ds = split(dfull[j:, j : j + LANES])
        v = dot3((near[0][:, j:], near[1][:, j:]), ds)
        scl[r, :, j : j + LANES] = v[:rows_dev]
        scl[par, :, j : j + LANES] = v[rows_dev:]
    rcopy(scl.at[r], scl.at[r], s_scl.at[0], sib, c)
    rcopy(scl.at[par], scl.at[par], s_scl.at[1], sib, c)

    over_rows = ((0,), (0,))
    dz = split(dfull[pl.ds(pl.multiple_of(c * share, SUBLANES), share), :])
    lanes = lambda j: slice(j * LANES, (j + 1) * LANES)
    cut = lambda pair, j: (pair[0][:, lanes(j)], pair[1][:, lanes(j)])
    for core in range(2):
        @pl.when(k == core)
        def _():
            for b, (i, j) in enumerate(pairs[core]):
                gpart[lanes(b), :] = dot3(cut(dz, i), cut(dz, j), over_rows)

    def v_of(side):
        sigma = split(sq[side].reshape(n_r * rows_dev, block_rows))
        return sigma, split(wz[side].reshape(block_rows, width))

    for j in others:
        wait_recv(wz.at[0, j], s_w.at[j])
    vpart[...] = dot3(*v_of(0))
    wait_recv(sq.at[1], s_sx.at[0])
    for j in others:
        wait_recv(wz.at[1, j], s_w.at[n_c + j])
    sigma, ws = v_of(1)
    for h in range(2):
        cols = slice(h * half, (h + 1) * half)
        vpart[:, cols] = vpart[:, cols] + dot3(sigma, (ws[0][:, cols], ws[1][:, cols]))
        rcopy(vpart.at[:, cols], vrecv.at[:, cols], s_v.at[h], sib, c)

    wait_recv(scl.at[sib], s_scl.at[0])
    wait_recv(scl.at[dia], s_scl.at[1])
    all_scl = split(scl[...].reshape(n_r * rows_dev, width))
    mask = jnp.concatenate([mask_of((rr * n_c + c) * rows_dev, rows_dev, x) for rr in range(n_r)], axis=0)
    for h in range(2):
        wait_recv(vrecv.at[:, slice(h * half, (h + 1) * half)], s_v.at[h])
    vs = split((vpart[...] + vrecv[...]) * mask)
    for core in range(2):
        @pl.when(k == core)
        def _():
            ofs = {}
            for slot, j in enumerate(columns[core]):
                at = j * LANES
                v = dot3((vs[0][:, at:], vs[1][:, at:]), split(dfull[at:, at : at + LANES]))
                of[slot] = v.reshape(n_r, rows_dev, LANES)
                ofs[j] = split(v)
            for b, (i, j) in enumerate(pairs[core]):
                left, right = (cut(all_scl, i), ofs[j]) if j in ofs else (ofs[i], cut(all_scl, j))
                gpart[lanes(b), :] += dot3(left, right, over_rows)

    rows_at = lambda j: pl.ds(pl.multiple_of(j * q, SUBLANES), q)
    for j in others:
        rcopy(gpart.at[rows_at(j), :], hrecv.at[c], s_h.at[c], r, j)
    for i, row in enumerate((sib, par, dia)):
        rcopy(of.at[:, row], offr.at[i], s_off.at[i], row, c)

    total = gpart[rows_at(c), :]
    for j in others:
        wait_recv(hrecv.at[j], s_h.at[j])
        total = total + hrecv[j]
    chunk = lambda s, core, j: res.at[s, core, rows_at(j), :]
    res[x, k, rows_at(c), :] = total

    mine = chunk(x, k, c)
    for j in others:
        rcopy(mine, mine, s_zag.at[c], r, j)

    def pass_on(j):
        got = chunk(x, k, j)
        rcopy(got, got, s_xag.at[j], par, c)
        rcopy(got, got, s_sib.at[x * n_c + j], sib, c)

    pass_on(c)

    def put_off(core, s, value):
        for slot, t in enumerate(columns[core]):
            at = pl.ds(t * supers + s, rows_dev, stride=nb * supers)
            off_ref[at, :] = -value(slot)

    for i in range(3):
        wait_recv(offr.at[i], s_off.at[i])
    for core in range(2):
        @pl.when(k == core)
        def _():
            put_off(core, x, lambda slot: of[slot, r])
            put_off(1 - core, x, lambda slot: offr[0, slot])
            put_off(core, 1 - x, lambda slot: offr[1, slot])
            put_off(1 - core, 1 - x, lambda slot: offr[2, slot])

    for j in others:
        wait_recv(chunk(x, k, j), s_zag.at[j])
        pass_on(j)
    for j in [c] + others:
        got = chunk(1 - x, k, j)
        wait_recv(got, s_xag.at[j])
        rcopy(got, got, s_sib.at[(1 - x) * n_c + j], sib, c)
    for s in range(supers):
        for j in range(n_c):
            wait_recv(chunk(s, 1 - k, j), s_sib.at[s * n_c + j])

    for cp in sends:
        cp.wait_send()
    for rr in range(n_r):
        @pl.when(r == rr)
        def _():
            copy_to(d_src(rr, 1 - x), d_slice(rr), s_d.at[rr], par, c, 0).wait_send()
            copy_to(d_src(rr, x), d_slice(rr), s_d.at[rr], sib, c, 1).wait_send()

        @pl.when(rr == par)
        def _():
            copy_to(d_slice(rr), d_slice(rr), s_d.at[rr], sib, c, 2).wait_send()


def unpack_kernel(supers, nb, off_in, res, off_out, diag_out, stage, sems):
    copies = [pltpu.make_async_copy(off_in, off_out, sems.at[supers * nb])]
    copies[0].start()
    place = {pair: (core, b) for core, some in enumerate(pairs_of(nb)) for b, pair in enumerate(some)}
    for s in range(supers):
        for i in range(nb):
            for j in range(nb):
                core, b = place[max(i, j), min(i, j)]
                v = res[s, core, b * LANES : (b + 1) * LANES, :]
                stage[s, i * LANES : (i + 1) * LANES, j * LANES : (j + 1) * LANES] = v if i >= j else jnp.transpose(v)
            at = (s, pl.ds(i * LANES, LANES))
            copies.append(pltpu.make_async_copy(stage.at[at], diag_out.at[at], sems.at[s * nb + i]))
            copies[-1].start()
    for cp in copies:
        cp.wait()


def fused_body(sigma_anc, anc_factor, diag_inverse, pattern):
    rows_dev, supers, width = anc_factor.shape
    n_r = lax.axis_size("row")
    n_c = lax.axis_size("col")
    total_rows = rows_dev * n_r * n_c
    nb = width // LANES
    packed = len(pairs_of(nb)[0]) * LANES
    q = packed // n_c
    slots = len(columns_of(nb)[0])
    f32 = lambda *shape: pltpu.VMEM(shape, jnp.float32)
    dma = lambda n: pltpu.SemaphoreType.DMA((n,))
    vm = pl.BlockSpec(memory_space=pltpu.VMEM)
    linear = jnp.transpose(anc_factor.reshape(rows_dev, supers, nb, LANES), (0, 2, 1, 3))
    linear = linear.reshape(rows_dev * nb * supers, LANES)
    off, res = pl.pallas_call(
        functools.partial(fused_kernel, n_r, n_c, supers, width, rows_dev, total_rows // pattern.shape[1]),
        out_shape=(
            pltpu.VMEM((rows_dev * supers * nb, LANES), jnp.float32),
            pltpu.VMEM((supers, 2, packed, LANES), jnp.float32),
        ),
        in_specs=[vm, vm, vm, pl.BlockSpec(memory_space=pltpu.SMEM)],
        out_specs=(vm, vm),
        scratch_shapes=[
            f32(supers, rows_dev, width),
            f32(n_r * rows_dev, n_c * rows_dev),
            f32(2, n_c, rows_dev, width),
            f32(2, n_c, rows_dev, n_c * rows_dev),
            f32(width, width),
            f32(n_r, rows_dev, width),
            f32(n_r * rows_dev, width),
            f32(n_r * rows_dev, width),
            f32(slots, n_r, rows_dev, LANES),
            f32(3, slots, rows_dev, LANES),
            f32(packed, LANES),
            f32(n_c, q, LANES),
            dma(16 + 12 * n_c),
            dma(2 * n_c), dma(n_c), dma(1), dma(n_r), dma(2), dma(2), dma(3), dma(n_c), dma(n_c), dma(n_c),
            dma(supers * n_c), dma(2),
        ],
        compiler_params=pltpu.CompilerParams(
            collective_id=0, has_side_effects=True, vmem_limit_bytes=48 * 1024 * 1024
        ),
    )(sigma_anc, linear, diag_inverse, pattern)
    hbm = pl.BlockSpec(memory_space=pl.ANY)
    off, diag = pl.pallas_call(
        functools.partial(unpack_kernel, supers, nb),
        out_shape=(
            jax.ShapeDtypeStruct(off.shape, jnp.float32),
            jax.ShapeDtypeStruct((supers, width, width), jnp.float32),
        ),
        in_specs=[vm, vm],
        out_specs=(hbm, hbm),
        scratch_shapes=[f32(supers, width, width), dma(supers * nb + 1)],
        compiler_params=pltpu.CompilerParams(vmem_limit_bytes=8 * 1024 * 1024),
    )(off, res)
    off = jnp.transpose(off.reshape(rows_dev, nb, supers, LANES), (0, 2, 1, 3))
    return off.reshape(anc_factor.shape), diag


def fits(sigma_anc, anc_factor, diag_inverse):
    rows_dev, supers, width = anc_factor.shape
    n_r = lax.axis_size("row")
    n_c = lax.axis_size("col")
    nb = width // LANES
    return (
        n_r == n_c
        and n_r == 2 * supers
        and supers == 2
        and sigma_anc.shape[0] == sigma_anc.shape[1]
        and diag_inverse.shape[2] % LANES == 0
        and nb % 4 == 0
        and rows_dev % SUBLANES == 0
        and width % (n_c * SUBLANES) == 0
        and len(pairs_of(nb)[0]) == len(pairs_of(nb)[1])
        and (len(pairs_of(nb)[0]) * LANES) % (n_c * SUBLANES) == 0
    )


def plain_body(sigma_anc, anc_factor, diag_inverse, pattern):
    precise = lax.Precision.HIGHEST
    rows_dev, supers, super_width = anc_factor.shape
    row_count = lax.axis_size("row")
    col_count = lax.axis_size("col")
    position = lax.axis_index("row") * col_count + lax.axis_index("col")
    total_rows = rows_dev * row_count * col_count
    block_size = total_rows // pattern.shape[1]
    flat_mask = jnp.repeat(pattern.astype(jnp.float32), block_size, axis=1)
    own_mask = jnp.transpose(lax.dynamic_slice_in_dim(flat_mask, position * rows_dev, rows_dev, 1))[
        :, :, None
    ]
    device_total = row_count * col_count
    share = -(-super_width // device_total)
    masked_factor = anc_factor * own_mask
    flattened = masked_factor.reshape(rows_dev, -1)
    gathered = lax.all_gather(flattened, "row", axis=0, tiled=True)
    stacked = gathered.reshape(row_count, rows_dev, flattened.shape[1])
    turned = lax.all_to_all(stacked, "col", split_axis=0, concat_axis=1, tiled=True)
    column_block = turned.reshape(row_count * rows_dev, flattened.shape[1])
    summed_rows = lax.psum_scatter(
        jnp.dot(sigma_anc, column_block, precision=precise, preferred_element_type=jnp.float32),
        "col",
        scatter_dimension=0,
        tiled=True,
    )
    off_factor = -(summed_rows.reshape(masked_factor.shape) * own_mask)
    both_rows = jnp.concatenate([masked_factor, off_factor], axis=0)
    column_piece = lax.all_gather(diag_inverse, "row", axis=2, tiled=True)
    product = jnp.einsum("rsk,skj->rsj", both_rows, column_piece, precision=precise)
    own_rows = lax.dynamic_slice_in_dim(column_piece, position * share, share, 1)
    scaled = product[:rows_dev]
    sel_off = product[rows_dev:]
    diag_term = jnp.einsum("skj,skl->sjl", own_rows, own_rows, precision=precise)
    partial_value = diag_term - jnp.einsum("rsj,rsl->sjl", scaled, sel_off, precision=precise)
    sel_diag = lax.psum(partial_value, ("row", "col"))
    return (sel_off, sel_diag)


def body(sigma_anc, anc_factor, diag_inverse, pattern):
    run = fused_body if fits(sigma_anc, anc_factor, diag_inverse) else plain_body
    return run(sigma_anc, anc_factor, diag_inverse, pattern)


def solution(mesh):
    return jax.shard_map(
        body,
        mesh=mesh,
        in_specs=(
            P(("grp", "row"), "col"),
            P(("grp", "row", "col"), None, None),
            P("grp", None, "row"),
            P(),
        ),
        out_specs=(P(("grp", "row", "col"), None, None), P("grp", None, None)),
        check_vma=False,
    )
```

time: 62.6 us -> 60.2 us (0.962)
  the two profiles are of different devices: /device:TPU:13 before, /device:TPU:0 now
where the time goes in v2:
time: 60.2 us; the launch traced here: 59.9 us
  Pallas kernels  55.7 us (93%)
  local copies, waits for them, and re-layouts  3.57 us (6%)
  between operations  0.65 us (1%)
    pallas_call x1, Pallas kernels, fused_body(): pl.pallas_call(functools.partial(fused_kernel, n_r, n_c, supers, width, r...  54.2 us
    unnamed x8, local copies, waits for them, and re-layouts  3.57 us
    pallas_call x1, Pallas kernels, fused_body(): pl.pallas_call(functools.partial(unpack_kernel, supers, nb), out_shape=(j...  1.52 us

profile of v2, /device:TPU:0, one launch (start us, length us, event | category | flops | bytes accessed | tf_op | source)
XLA Modules:
  0.0 59.9 jit_solution(16789093572037167931)
XLA Ops:
  0.6 0.0 copy-start
  0.6 1.0 %copy-done = f32[2,512,128]{2,1,0:T(8,128)S(1)} copy-done((f32[2,512,128]{2,1,0:T(8,128)S(1)}, f32[2,512,128]{2,1,0:T(8,128)}, u32[]{:S(2)}) %copy-start) | copy-done | bytes 524312
  1.7 0.0 copy-start.1
  1.7 0.9 %copy-done.1 = f32[192,192]{1,0:T(8,128)S(1)} copy-done((f32[192,192]{1,0:T(8,128)S(1)}, f32[192,192]{1,0:T(8,128)}, u32[]{:S(2)}) %copy-start.1) | copy-done | bytes 147480
  2.6 0.0 copy-start.2
  2.6 0.9 %copy-done.2 = f32[48,2,512]{2,1,0:T(2,128)S(1)} copy-done((f32[48,2,512]{2,1,0:T(2,128)S(1)}, f32[48,2,512]{2,1,0:T(2,128)}, u32[]{:S(2)}) %copy-start.2) | copy-done | bytes 196632
  3.5 0.0 copy-start.3
  3.5 0.7 %copy-done.3 = s32[2,6]{1,0:T(2,128)S(1)} copy-done((s32[2,6]{1,0:T(2,128)S(1)}, s32[2,6]{1,0:T(2,128)}, u32[]{:S(2)}) %copy-start.3) | copy-done | bytes 72
  4.2 54.2 %shard_map.59 = (f32[384,128]{1,0:T(8,128)S(1)}, f32[2,2,640,128]{3,2,1,0:T(8,128)S(1)}) custom-call(f32[192,192]{1,0:T(8,128)S(1)} %copy-done.1, f32[384,128]{1,0:T(8,128)S(1)} %bitcast.10, f32[2,512,128]{2,1,0:T(8,128)S(1)} %copy-done, s32[2,6]{1,0:T(2,128)S(1)} %copy-done.3), custom_call_target="tpu_custom_call" | custom-call | tf_op jit(solution)/shard_map/pallas_call | solution.py:300
  58.4 1.5 %shard_map.60 = (f32[384,128]{1,0:T(8,128)}, f32[2,512,512]{2,1,0:T(8,128)}) custom-call(f32[384,128]{1,0:T(8,128)S(1)} %get-tuple-element.6.off_in, f32[2,2,640,128]{3,2,1,0:T(8,128)S(1)} %get-tuple-element.7.res), custom_call_target="tpu_custom_call" | custom-call | tf_op jit(solution)/shard_map/pallas_call | solution.py:330
Async XLA Ops:
  0.6 1.0 %copy-start = (f32[2,512,128]{2,1,0:T(8,128)S(1)}, f32[2,512,128]{2,1,0:T(8,128)}, u32[]{:S(2)}) copy-start(f32[2,512,128]{2,1,0:T(8,128)} %d_ref.1) | copy-start | bytes 1572868
  1.7 0.9 %copy-start.1 = (f32[192,192]{1,0:T(8,128)S(1)}, f32[192,192]{1,0:T(8,128)}, u32[]{:S(2)}) copy-start(f32[192,192]{1,0:T(8,128)} %sig_ref.1) | copy-start | bytes 442372
  2.6 0.9 %copy-start.2 = (f32[48,2,512]{2,1,0:T(2,128)S(1)}, f32[48,2,512]{2,1,0:T(2,128)}, u32[]{:S(2)}) copy-start(f32[48,2,512]{2,1,0:T(2,128)} %param.5) | copy-start | bytes 589828
  3.5 0.7 %copy-start.3 = (s32[2,6]{1,0:T(2,128)S(1)}, s32[2,6]{1,0:T(2,128)}, u32[]{:S(2)}) copy-start(s32[2,6]{1,0:T(2,128)} %pat_ref.1) | copy-start | bytes 148

commit v3 on v2

--- a/solution.py
+++ b/solution.py
@@ -39,10 +39,10 @@
 
 def fused_kernel(
     n_r, n_c, supers, width, rows_dev, block_size,
-    sig_ref, a_ref, d_ref, pat_ref,
+    sig_hbm, a_hbm, d_ref, pat_ref,
     off_ref, res,
-    av, sig_t, wz, sq, dfull, scl, vpart, vrecv, of, offr, gpart, hrecv,
-    send_sems, s_w, s_sq, s_sx, s_d, s_scl, s_v, s_off, s_h, s_zag, s_xag, s_sib, local_sems,
+    sig_ref, a_ref, av, sig_t, wz, sq, dfull, scl, vpart, vrecv, of, offr, gpart, hrecv, hjoin, hjrecv,
+    send_sems, s_w, s_sq, s_sx, s_d, s_scl, s_v, s_off, s_h, s_hj, s_zag, s_xag, s_far, s_sib, local_sems,
 ):
     r = lax.axis_index("row")
     c = lax.axis_index("col")
@@ -68,15 +68,53 @@
         )
 
     first_slot = 4
+    z_slot = first_slot + 4 * n_c + 12
+    done = [0] * (n_c + 1)
 
     def rcopy(src, dst, rsem, row, col):
         cp = copy_to(src, dst, rsem, row, col, first_slot + len(sends))
         cp.start()
         sends.append(cp)
 
+    plans = [[] for _ in range(n_c)]
+
+    def at_each_col(f):
+        for cc in range(n_c):
+            pl.when(c == cc)(functools.partial(f, cc))
+
+    def post(cc, refs, row, col):
+        slot = z_slot + len(plans[cc])
+        make = lambda: copy_to(*refs(), row, col, slot)
+        make().start()
+        plans[cc].append(make)
+
+    def wait_sends():
+        for cp in sends[done[0] :]:
+            cp.wait_send()
+        done[0] = len(sends)
+
+        def at(cc):
+            for make in plans[cc][done[1 + cc] :]:
+                make().wait_send()
+            done[1 + cc] = len(plans[cc])
+
+        at_each_col(at)
+
+    def giver(j, t):
+        edge = j in (0, n_c - 1)
+        return j if abs(j - t) == 1 or (edge and abs(j - t) == 2) else t + (1 if j > t else -1)
+
+    by_distance = lambda cc: sorted((j for j in range(n_c) if j != cc), key=lambda j: abs(j - cc))
+
     def wait_recv(dst, rsem):
         pltpu.make_async_copy(dst, dst, rsem).wait()
 
+    loads = [
+        pltpu.make_async_copy(a_hbm, a_ref, local_sems.at[2]),
+        pltpu.make_async_copy(sig_hbm, sig_ref, local_sems.at[3]),
+    ]
+    for cp in loads:
+        cp.start()
     others = [(c + dc) % n_c for dc in range(1, n_c)]
     barrier = pltpu.get_barrier_semaphore()
     sig = lambda row, col: pl.semaphore_signal(
@@ -95,21 +133,41 @@
             m = jnp.where(inside, pat_ref[s, b].astype(jnp.float32), m)
         return m
 
+    loads[0].wait()
     for s in range(supers):
         mask = mask_of((r * n_c + c) * rows_dev, rows_dev, s)
         for t in range(nb):
             rows = a_ref[pl.ds(t * supers + s, rows_dev, stride=nb * supers), :]
             av[s, :, t * LANES : (t + 1) * LANES] = rows * mask
+    loads[1].wait()
     sig_t[...] = jnp.transpose(sig_ref[...])
 
     pl.semaphore_wait(barrier, n_c + 2)
 
     sig_rows = lambda j: pl.ds(pl.multiple_of(j * rows_dev, SUBLANES), rows_dev)
     rcopy(av.at[1 - x], wz.at[1, c], s_w.at[n_c + c], par, c)
-    for j in others:
-        rcopy(sig_t.at[sig_rows(j), :], sq.at[0, c], s_sq.at[c], r, j)
-    for j in others:
-        rcopy(av.at[x], wz.at[0, c], s_w.at[c], r, j)
+
+    row_block = lambda side, j: (wz.at[side, j], s_w.at[side * n_c + j])
+
+    def spread(cc, src, side):
+        for t in by_distance(cc):
+            if giver(cc, t) == cc:
+                post(cc, lambda: (src(), *row_block(side, cc)), r, t)
+
+    def pass_rows(cc, side, upto):
+        for j in by_distance(cc):
+            if (abs(j - cc) == 1) == upto:
+                wait_recv(*row_block(side, j))
+                for t in range(n_c):
+                    if t not in (j, cc) and giver(j, t) == cc:
+                        post(cc, lambda j=j: (wz.at[side, j], *row_block(side, j)), r, t)
+
+    def send_first(cc):
+        for j in by_distance(cc):
+            post(cc, lambda j=j: (sig_t.at[sig_rows(j), :], sq.at[0, cc], s_sq.at[cc]), r, j)
+        spread(cc, lambda: av.at[x], 0)
+
+    at_each_col(send_first)
     own_copy = pltpu.make_async_copy(av.at[x], wz.at[0, c], local_sems.at[1])
     own_copy.start()
 
@@ -127,17 +185,19 @@
         dfull[0 : rr * piece, rr * piece : (rr + 1) * piece] = jnp.zeros((rr * piece, piece), jnp.float32)
 
     wait_recv(wz.at[1, c], s_w.at[n_c + c])
-    for j in others:
-        rcopy(wz.at[1, c], wz.at[1, c], s_w.at[n_c + c], r, j)
+    at_each_col(lambda cc: spread(cc, lambda: wz.at[1, cc], 1))
     for j in others:
         wait_recv(sq.at[0, j], s_sq.at[j])
     rcopy(sq.at[0], sq.at[1], s_sx.at[0], par, c)
+    at_each_col(lambda cc: pass_rows(cc, 0, True))
+    at_each_col(lambda cc: pass_rows(cc, 0, False))
 
     for rr in range(n_r):
         @pl.when(rr == par)
         def _():
             wait_recv(d_slice(rr), s_d.at[rr])
             copy_to(d_slice(rr), d_slice(rr), s_d.at[rr], sib, c, 2).start()
+    at_each_col(lambda cc: pass_rows(cc, 1, True))
     for rr in range(n_r):
         @pl.when((rr == sib) | (rr == dia))
         def _():
@@ -171,12 +231,9 @@
         sigma = split(sq[side].reshape(n_r * rows_dev, block_rows))
         return sigma, split(wz[side].reshape(block_rows, width))
 
-    for j in others:
-        wait_recv(wz.at[0, j], s_w.at[j])
     vpart[...] = dot3(*v_of(0))
     wait_recv(sq.at[1], s_sx.at[0])
-    for j in others:
-        wait_recv(wz.at[1, j], s_w.at[n_c + j])
+    at_each_col(lambda cc: pass_rows(cc, 1, False))
     sigma, ws = v_of(1)
     for h in range(2):
         cols = slice(h * half, (h + 1) * half)
@@ -204,28 +261,56 @@
                 gpart[lanes(b), :] += dot3(left, right, over_rows)
 
     rows_at = lambda j: pl.ds(pl.multiple_of(j * q, SUBLANES), q)
-    for j in others:
-        rcopy(gpart.at[rows_at(j), :], hrecv.at[c], s_h.at[c], r, j)
+
+    joined = lambda j, t: j in (0, n_c - 1) and abs(j - t) == 2
+
+    def scatter(cc):
+        targets = sorted((t for t in range(n_c) if t != cc), key=lambda t: (not joined(cc, t), -abs(t - cc)))
+        late = [t for t in targets if any(joined(j, t) and (j + t) // 2 == cc for j in range(n_c))]
+        for t in targets:
+            if joined(cc, t):
+                post(cc, lambda t=t: (gpart.at[rows_at(t), :], hrecv.at[t], s_h.at[t]), r, (cc + t) // 2)
+            elif t not in late:
+                post(cc, lambda t=t: (gpart.at[rows_at(t), :], hrecv.at[cc], s_h.at[cc]), r, t)
+        for t in late:
+            wait_recv(hrecv.at[t], s_h.at[t])
+            hjoin[...] = gpart[rows_at(t), :] + hrecv[t]
+            post(cc, lambda: (hjoin, hjrecv, s_hj.at[0]), r, t)
+
+    at_each_col(scatter)
     for i, row in enumerate((sib, par, dia)):
         rcopy(of.at[:, row], offr.at[i], s_off.at[i], row, c)
 
+    wait_sends()
+    mine_at = lambda: gpart.at[rows_at(c), :]
+
+    def collect(cc):
+        for j in by_distance(cc):
+            if joined(j, cc):
+                continue
+            if any(joined(i, cc) and (i + cc) // 2 == j for i in range(n_c)):
+                wait_recv(hjrecv, s_hj.at[0])
+                mine_at()[...] += hjrecv[...]
+            else:
+                wait_recv(hrecv.at[j], s_h.at[j])
+                mine_at()[...] += hrecv[j]
+
+    at_each_col(collect)
     total = gpart[rows_at(c), :]
-    for j in others:
-        wait_recv(hrecv.at[j], s_h.at[j])
-        total = total + hrecv[j]
     chunk = lambda s, core, j: res.at[s, core, rows_at(j), :]
     res[x, k, rows_at(c), :] = total
 
     mine = chunk(x, k, c)
-    for j in others:
-        rcopy(mine, mine, s_zag.at[c], r, j)
-
-    def pass_on(j):
-        got = chunk(x, k, j)
-        rcopy(got, got, s_xag.at[j], par, c)
-        rcopy(got, got, s_sib.at[x * n_c + j], sib, c)
-
-    pass_on(c)
+    rcopy(mine, mine, s_xag.at[c], par, c)
+
+    def gather(cc):
+        for t in by_distance(cc):
+            if giver(cc, t) == cc:
+                post(cc, lambda: (chunk(x, k, cc), chunk(x, k, cc), s_zag.at[cc]), r, t)
+
+    at_each_col(gather)
+    rcopy(mine, mine, s_sib.at[x * n_c + c], sib, c)
+    opposite = n_c - 1 - c
 
     def put_off(core, s, value):
         for slot, t in enumerate(columns[core]):
@@ -242,19 +327,36 @@
             put_off(core, 1 - x, lambda slot: offr[1, slot])
             put_off(1 - core, 1 - x, lambda slot: offr[2, slot])
 
-    for j in others:
-        wait_recv(chunk(x, k, j), s_zag.at[j])
-        pass_on(j)
-    for j in [c] + others:
-        got = chunk(1 - x, k, j)
-        wait_recv(got, s_xag.at[j])
-        rcopy(got, got, s_sib.at[(1 - x) * n_c + j], sib, c)
+    away = 1 - x
+    theirs = chunk(away, k, c)
+    wait_recv(theirs, s_xag.at[c])
+    rcopy(theirs, theirs, s_far.at[c], r, opposite)
+    rcopy(theirs, theirs, s_sib.at[(1 - x) * n_c + c], sib, c)
+
+    def pass_on(cc):
+        for j in by_distance(cc):
+            got = chunk(x, k, j)
+            wait_recv(got, s_zag.at[j])
+            for t in range(n_c):
+                if t not in (j, cc) and giver(j, t) == cc:
+                    post(cc, lambda j=j: (chunk(x, k, j), chunk(x, k, j), s_zag.at[j]), r, t)
+            if j != n_c - 1 - cc:
+                forward(cc, x, j, lambda j=j: s_xag.at[j], par)
+            forward(cc, x, j, lambda j=j: s_sib.at[x * n_c + j], sib)
+        for j in by_distance(cc):
+            got = chunk(1 - x, k, j)
+            wait_recv(got, s_far.at[j] if j == n_c - 1 - cc else s_xag.at[j])
+            forward(cc, away, j, lambda j=j: s_sib.at[away * n_c + j], sib)
+
+    def forward(cc, s, j, rsem, row):
+        post(cc, lambda: (chunk(s, k, j), chunk(s, k, j), rsem()), row, c)
+
+    at_each_col(pass_on)
     for s in range(supers):
         for j in range(n_c):
             wait_recv(chunk(s, 1 - k, j), s_sib.at[s * n_c + j])
 
-    for cp in sends:
-        cp.wait_send()
+    wait_sends()
     for rr in range(n_r):
         @pl.when(r == rr)
         def _():
@@ -297,15 +399,18 @@
     vm = pl.BlockSpec(memory_space=pltpu.VMEM)
     linear = jnp.transpose(anc_factor.reshape(rows_dev, supers, nb, LANES), (0, 2, 1, 3))
     linear = linear.reshape(rows_dev * nb * supers, LANES)
+    hbm = pl.BlockSpec(memory_space=pl.ANY)
     off, res = pl.pallas_call(
         functools.partial(fused_kernel, n_r, n_c, supers, width, rows_dev, total_rows // pattern.shape[1]),
         out_shape=(
             pltpu.VMEM((rows_dev * supers * nb, LANES), jnp.float32),
             pltpu.VMEM((supers, 2, packed, LANES), jnp.float32),
         ),
-        in_specs=[vm, vm, vm, pl.BlockSpec(memory_space=pltpu.SMEM)],
+        in_specs=[hbm, hbm, hbm, pl.BlockSpec(memory_space=pltpu.SMEM)],
         out_specs=(vm, vm),
         scratch_shapes=[
+            f32(*sigma_anc.shape),
+            f32(*linear.shape),
             f32(supers, rows_dev, width),
             f32(n_r * rows_dev, n_c * rows_dev),
             f32(2, n_c, rows_dev, width),
@@ -318,15 +423,16 @@
             f32(3, slots, rows_dev, LANES),
             f32(packed, LANES),
             f32(n_c, q, LANES),
-            dma(16 + 12 * n_c),
-            dma(2 * n_c), dma(n_c), dma(1), dma(n_r), dma(2), dma(2), dma(3), dma(n_c), dma(n_c), dma(n_c),
-            dma(supers * n_c), dma(2),
+            f32(q, LANES),
+            f32(q, LANES),
+            dma(16 + 24 * n_c),
+            dma(2 * n_c), dma(n_c), dma(1), dma(n_r), dma(2), dma(2), dma(3), dma(n_c), dma(1), dma(n_c), dma(n_c), dma(n_c),
+            dma(supers * n_c), dma(4),
         ],
         compiler_params=pltpu.CompilerParams(
-            collective_id=0, has_side_effects=True, vmem_limit_bytes=48 * 1024 * 1024
+            collective_id=0, has_side_effects=True, vmem_limit_bytes=58 * 1024 * 1024
         ),
     )(sigma_anc, linear, diag_inverse, pattern)
-    hbm = pl.BlockSpec(memory_space=pl.ANY)
     off, diag = pl.pallas_call(
         functools.partial(unpack_kernel, supers, nb),
         out_shape=(

time: 60.2 us -> 55.7 us (0.925)
  local copies, waits for them, and re-layouts: 3.57 us -> 0 us
  Pallas kernels: 55.7 us -> 54.9 us
    unnamed x8 -> x0, local copies, waits for them, and re-layouts: 3.57 us -> none
    pallas_call x1, Pallas kernels: 54.2 us -> 53.4 us  [fused_body(): pl.pallas_call(functools.partial(fused_kernel, n_r, n_c, supers, width, r...]
where the time goes in v3:
time: 55.7 us; the launch traced here: 55.6 us
  Pallas kernels  54.9 us (99%)
  between operations  0.64 us (1%)
    pallas_call x1, Pallas kernels, fused_body(): pl.pallas_call(functools.partial(fused_kernel, n_r, n_c, supers, width, r...  53.4 us
    pallas_call x1, Pallas kernels, fused_body(): pl.pallas_call(functools.partial(unpack_kernel, supers, nb), out_shape=(j...  1.52 us

profile of v3, /device:TPU:0, one launch (start us, length us, event | category | flops | bytes accessed | tf_op | source)
XLA Modules:
  0.0 55.6 jit_solution(12188072585820508798)
XLA Ops:
  0.6 53.4 %shard_map.59 = (f32[384,128]{1,0:T(8,128)S(1)}, f32[2,2,640,128]{3,2,1,0:T(8,128)S(1)}) custom-call(f32[192,192]{1,0:T(8,128)} %sig_hbm.1, f32[384,128]{1,0:T(8,128)} %bitcast.10, f32[2,512,128]{2,1,0:T(8,128)} %d_ref.1, s32[2,6]{1,0:T(2,128)} %pat_ref.1), custom_call_target="tpu_custom_call" | custom-call | tf_op jit(solution)/shard_map/pallas_call | solution.py:403
  54.0 1.5 %shard_map.60 = (f32[384,128]{1,0:T(8,128)}, f32[2,512,512]{2,1,0:T(8,128)}) custom-call(f32[384,128]{1,0:T(8,128)S(1)} %get-tuple-element.6.off_in, f32[2,2,640,128]{3,2,1,0:T(8,128)S(1)} %get-tuple-element.7.res), custom_call_target="tpu_custom_call" | custom-call | tf_op jit(solution)/shard_map/pallas_call | solution.py:436

commit v4 on v2

v4 whole, which is shorter than its diff:
```python
import functools

import jax
import jax.numpy as jnp
from jax import lax
from jax.experimental import pallas as pl
from jax.experimental.pallas import tpu as pltpu
from jax.sharding import PartitionSpec as P

LANES = 128
SUBLANES = 8
PARTS = 4


def split(x):
    high = x.astype(jnp.bfloat16)
    low = (x - high.astype(jnp.float32)).astype(jnp.bfloat16)
    return high, low


def dot3(a, b, contract=((1,), (0,))):
    (ah, al), (bh, bl) = a, b
    f = lambda u, v: lax.dot_general(u, v, (contract, ((), ())), preferred_element_type=jnp.float32)
    return f(ah, bh) + (f(ah, bl) + f(al, bh))


def columns_of(nb):
    return [[j for j in range(nb) if (j + j // 2) % 2 == core] for core in range(2)]


def pairs_of(nb):
    columns = columns_of(nb)
    pairs = [[], []]
    every = [(i, j) for i in range(nb) for j in range(i + 1)]
    owners = lambda pair: [core for core in range(2) if pair[0] in columns[core] or pair[1] in columns[core]]
    for pair in sorted(every, key=lambda p: len(owners(p))):
        pairs[min(owners(pair), key=lambda core: len(pairs[core]))].append(pair)
    return pairs


def fused_kernel(
    n_r, n_c, supers, width, rows_dev, block_size, parts,
    sig_hbm, a_hbm, d_ref, pat_ref,
    off_ref, res,
    sig_ref, a_ref, av, sig_t, wz, sq, dfull, scl, vpart, vrecv, of, offr, gpart, grecv,
    send_sems, s_w, s_sq, s_d, s_scl, s_v, s_off, s_h, s_g, s_sib, local_sems,
):
    r = lax.axis_index("row")
    c = lax.axis_index("col")
    x = r // 2
    k = r % 2
    away = 1 - x
    sib = 2 * x + 1 - k
    par = 2 * away + k
    dia = 2 * away + 1 - k
    piece = width // n_r
    nb = width // LANES
    block_rows = rows_dev * n_c
    side_rows = 2 * rows_dev
    columns = columns_of(nb)
    pairs = pairs_of(nb)
    q = len(pairs[0]) * LANES // (2 * parts)
    low = n_c // 2 - 1
    side = c // 2
    mate = 4 * side + 1 - c
    hub = low + side
    is_hub = hub == c
    is_edge = hub != c
    plans = [[] for _ in range(n_c)]
    done = [0] * n_c
    v_slot = 4
    z_slot = v_slot + nb

    def copy_to(src, dst, rsem, row, col, slot):
        return pltpu.make_async_remote_copy(
            src_ref=src, dst_ref=dst, send_sem=send_sems.at[slot], recv_sem=rsem,
            device_id={"row": row, "col": col}, device_id_type=pl.DeviceIdType.MESH,
        )

    def at_each_col(hub_part, edge_part=None):
        for cc in range(n_c):
            hub_col = low + cc // 2
            part = hub_part if cc == hub_col else edge_part
            if part is not None:
                pl.when(c == cc)(functools.partial(part, cc, n_c - 1 - cc))

    def post(cc, refs, row, col):
        slot = z_slot + len(plans[cc])
        make = lambda: copy_to(*refs(), row, col, slot)
        make().start()
        plans[cc].append(make)

    def wait_sends():
        def at(cc, *_):
            for make in plans[cc][done[cc] :]:
                make().wait_send()
            done[cc] = len(plans[cc])

        at_each_col(at, at)

    def wait_recv(dst, rsem):
        pltpu.make_async_copy(dst, dst, rsem).wait()

    loads = [
        pltpu.make_async_copy(a_hbm, a_ref, local_sems.at[2]),
        pltpu.make_async_copy(sig_hbm, sig_ref, local_sems.at[3]),
    ]
    for cp in loads:
        cp.start()
    barrier = pltpu.get_barrier_semaphore()
    sig = lambda row, col: pl.semaphore_signal(
        barrier, inc=1, device_id={"row": row, "col": col}, device_id_type=pl.DeviceIdType.MESH
    )
    for dc in range(1, n_c):
        sig(r, (c + dc) % n_c)
    for row in (sib, par, dia):
        sig(row, c)
        sig(row, mate)

    def mask_of(first, rows, s):
        row = first + lax.broadcasted_iota(jnp.int32, (rows, 1), 0)
        m = jnp.zeros((rows, 1), jnp.float32)
        for b in range(pat_ref.shape[1]):
            inside = (row >= b * block_size) & (row < (b + 1) * block_size)
            m = jnp.where(inside, pat_ref[s, b].astype(jnp.float32), m)
        return m

    loads[0].wait()
    for s in range(supers):
        mask = mask_of((r * n_c + c) * rows_dev, rows_dev, s)
        for t in range(nb):
            rows = a_ref[pl.ds(t * supers + s, rows_dev, stride=nb * supers), :]
            av[s, :, t * LANES : (t + 1) * LANES] = rows * mask
    loads[1].wait()
    sig_t[...] = jnp.transpose(sig_ref[...])

    pl.semaphore_wait(barrier, n_c + 5)

    rows_w = lambda own, j: (wz.at[own, j], s_w.at[own * n_c + j])
    rows_s = lambda own, j: (sq.at[own, j], s_sq.at[own * n_c + j])
    half_of = lambda h: sig_t.at[pl.ds(h * side_rows, side_rows), :]
    d_slice = lambda rr: dfull.at[pl.ds(rr * piece, width - rr * piece), pl.ds(rr * piece, piece)]
    d_src = lambda rr, s: d_ref.at[s, pl.ds(rr * piece, width - rr * piece), :]
    sends_d = (is_hub & (k == 0)) | (is_edge & (k == 1))

    def hub_first(cc, other):
        post(cc, lambda: (av.at[away], *rows_w(1, cc)), par, c)
        post(cc, lambda: (half_of(1 - cc // 2), *rows_s(0, cc)), r, other)
        post(cc, lambda: (av.at[x], *rows_w(0, cc)), r, other)
        post(cc, lambda: (half_of(cc // 2), *rows_s(1, cc)), par, c)

    def edge_first(cc, other):
        near = low + cc // 2
        post(cc, lambda: (av.at[away], *rows_w(1, cc)), par, c)
        post(cc, lambda: (av.at[x], *rows_w(0, cc)), r, near)
        post(cc, lambda: (half_of(1 - cc // 2), *rows_s(0, cc)), r, n_c - 1 - near)
        post(cc, lambda: (half_of(cc // 2), *rows_s(0, cc)), r, near)

    at_each_col(hub_first, edge_first)
    for rr in range(n_r):
        @pl.when((r == rr) & sends_d)
        def _():
            copy_to(d_src(rr, away), d_slice(rr), s_d.at[rr], par, c, 0).start()

        @pl.when((r == rr) & is_hub)
        def _():
            copy_to(d_src(rr, x), d_slice(rr), s_d.at[rr], sib, c, 1).start()
            pltpu.make_async_copy(d_src(rr, x), d_slice(rr), local_sems.at[0]).start()

    @pl.when(is_hub)
    def _():
        wz[0, c] = av[x]
        sq[0, c] = sig_t[pl.ds(pl.multiple_of(side * side_rows, SUBLANES), side_rows), :]
        for rr in range(1, n_r):
            dfull[0 : rr * piece, rr * piece : (rr + 1) * piece] = jnp.zeros((rr * piece, piece), jnp.float32)

    def hub_pass(cc, other):
        edge = 0 if cc == low else n_c - 1
        wait_recv(*rows_w(1, cc))
        post(cc, lambda: (wz.at[1, cc], *rows_w(1, cc)), r, other)
        wait_recv(*rows_w(0, edge))
        post(cc, lambda: (wz.at[0, edge], *rows_w(0, edge)), r, other)
        for j in (other, edge, n_c - 1 - edge):
            wait_recv(*rows_s(0, j))
            post(cc, lambda j=j: (sq.at[0, j], *rows_s(1, j)), par, c)

    def hub_pass_last(cc, other):
        edge = 0 if cc == low else n_c - 1
        wait_recv(*rows_w(1, edge))
        post(cc, lambda: (wz.at[1, edge], *rows_w(1, edge)), r, other)

    def edge_pass(cc, other):
        wait_recv(*rows_w(1, cc))
        post(cc, lambda: (wz.at[1, cc], *rows_w(1, cc)), r, low + cc // 2)

    at_each_col(hub_pass, edge_pass)
    for rr in range(n_r):
        @pl.when((rr == par) & is_hub)
        def _():
            @pl.when(k == 0)
            def _():
                wait_recv(d_slice(rr), s_d.at[rr])
                copy_to(d_slice(rr), d_slice(rr), s_d.at[rr], sib, c, 2).start()

        @pl.when((rr == par) & is_edge & (k == 1))
        def _():
            wait_recv(d_slice(rr), s_d.at[rr])
            copy_to(d_slice(rr), d_slice(rr), s_d.at[rr], r, hub, 3).start()
    at_each_col(hub_pass_last)
    for rr in range(n_r):
        @pl.when((rr == par) & is_hub & (k == 1))
        def _():
            wait_recv(d_slice(rr), s_d.at[rr])
            copy_to(d_slice(rr), d_slice(rr), s_d.at[rr], sib, c, 2).start()
    for rr in range(n_r):
        @pl.when(((rr == sib) | (rr == dia)) & is_hub)
        def _():
            wait_recv(d_slice(rr), s_d.at[rr])

        @pl.when((rr == r) & is_hub)
        def _():
            pltpu.make_async_copy(d_src(rr, x), d_slice(rr), local_sems.at[0]).wait()

    over_rows = ((0,), (0,))
    lanes = lambda j: slice(j * LANES, (j + 1) * LANES)
    cut = lambda pair, j: (pair[0][:, lanes(j)], pair[1][:, lanes(j)])
    mask_rows = lambda: jnp.concatenate(
        [mask_of((rr * n_c + 2 * side) * rows_dev, side_rows, x) for rr in range(n_r)], axis=0
    )

    @pl.when(is_hub)
    def _():
        own = [wz[o, pl.ds(2 * side, 2)].reshape(side_rows, width) for o in range(2)]
        near = split(jnp.concatenate(own, axis=0))
        for j in range(0, width, LANES):
            ds = split(dfull[j:, j : j + LANES])
            v = dot3((near[0][:, j:], near[1][:, j:]), ds)
            scl[r, :, j : j + LANES] = v[:side_rows]
            scl[par, :, j : j + LANES] = v[side_rows:]

    def hub_scl(cc, *_):
        post(cc, lambda: (scl.at[r], scl.at[r], s_scl.at[0]), sib, c)
        post(cc, lambda: (scl.at[par], scl.at[par], s_scl.at[1]), sib, c)

    at_each_col(hub_scl)

    @pl.when(is_hub)
    def _():
        dz = split(dfull[pl.ds(pl.multiple_of(side * (width // 2), SUBLANES), width // 2), :])
        for core in range(2):
            @pl.when(k == core)
            def _():
                for b, (i, j) in enumerate(pairs[core]):
                    gpart[lanes(b), :] = dot3(cut(dz, i), cut(dz, j), over_rows)

    def v_of(own):
        sigma = split(sq[own].reshape(n_r * side_rows, block_rows))
        return sigma, split(wz[own].reshape(block_rows, width))

    def hub_wait(own, cc, other):
        edge = 0 if cc == low else n_c - 1
        for j in (other, n_c - 1 - edge):
            wait_recv(*rows_w(own, j))
        if own == 1:
            for j in range(n_c):
                wait_recv(*rows_s(1, j))

    at_each_col(functools.partial(hub_wait, 0))

    @pl.when(is_hub)
    def _():
        vpart[...] = dot3(*v_of(0))

    at_each_col(functools.partial(hub_wait, 1))
    v_cols = lambda h: slice(h * LANES, (h + 1) * LANES)

    @pl.when(is_hub)
    def _():
        sigma, ws = v_of(1)
        for h in range(nb):
            vpart[:, v_cols(h)] = vpart[:, v_cols(h)] + dot3(sigma, cut(ws, h))
            copy_to(vpart.at[:, v_cols(h)], vrecv.at[:, v_cols(h)], s_v.at[h], sib, c, v_slot + h).start()

        wait_recv(scl.at[sib], s_scl.at[0])
        wait_recv(scl.at[dia], s_scl.at[1])
        all_scl = split(scl[...].reshape(n_r * side_rows, width))
        for h in range(nb):
            wait_recv(vrecv.at[:, v_cols(h)], s_v.at[h])
        vs = split((vpart[...] + vrecv[...]) * mask_rows())
        for core in range(2):
            @pl.when(k == core)
            def _():
                ofs = {}
                for slot, j in enumerate(columns[core]):
                    at = j * LANES
                    v = dot3((vs[0][:, at:], vs[1][:, at:]), split(dfull[at:, at : at + LANES]))
                    of[slot] = v.reshape(n_r, 2, rows_dev, LANES)
                    ofs[j] = split(v)
                for b, (i, j) in enumerate(pairs[core]):
                    left, right = (cut(all_scl, i), ofs[j]) if j in ofs else (ofs[i], cut(all_scl, j))
                    gpart[lanes(b), :] += dot3(left, right, over_rows)

    rows_at = lambda h, i: pl.ds((h * parts + i) * q, q)
    chunk = lambda s, h, i: (res.at[s, k, rows_at(h, i), :], s_g.at[(s * 2 + h) * parts + i])
    held = lambda s, h, i: res.at[s, k, rows_at(h, i), :]

    def hub_scatter(cc, other):
        for i in range(parts):
            post(cc, lambda i=i: (gpart.at[rows_at(1 - cc // 2, i), :], grecv.at[i], s_h.at[i]), r, other)
        edge = 0 if cc == low else n_c - 1
        for row in (sib, par, dia):
            post(cc, lambda row=row: (of.at[:, row, cc - 2 * (cc // 2)], offr.at[r], s_off.at[r]), row, cc)
        for row in (r, sib, par, dia):
            post(cc, lambda row=row: (of.at[:, row, edge - 2 * (cc // 2)], offr.at[r], s_off.at[r]), row, edge)
        pltpu.make_async_copy(of.at[:, r, cc - 2 * (cc // 2)], offr.at[r], s_off.at[r]).start()

    at_each_col(hub_scatter)
    wait_sends()

    def forward(cc, s, h, i, row, col):
        post(cc, lambda: (held(s, h, i), *chunk(s, h, i)), row, col)

    def to_sib(cc, s, h, i):
        post(cc, lambda: (held(s, h, i), held(s, h, i), s_sib.at[(s * 2 + h) * parts + i]), sib, c)

    def hub_reduce(cc, other):
        h = cc // 2
        edge = 0 if cc == low else n_c - 1
        for i in range(parts):
            wait_recv(grecv.at[i], s_h.at[i])
            res[x, k, rows_at(h, i), :] = gpart[rows_at(h, i), :] + grecv[i]
            forward(cc, x, h, i, par, c)
            forward(cc, x, h, i, r, other)
            forward(cc, x, h, i, r, edge)
            to_sib(cc, x, h, i)

    at_each_col(hub_reduce)

    for row in range(n_r):
        wait_recv(offr.at[row], s_off.at[row])
        for slot, t in enumerate(columns[row % 2]):
            at = pl.ds(t * supers + row // 2, rows_dev, stride=nb * supers)
            off_ref[at, :] = -offr[row, slot]

    def hub_gather(cc, other):
        h = cc // 2
        edge = 0 if cc == low else n_c - 1
        for i in range(parts):
            wait_recv(*chunk(x, 1 - h, i))
            forward(cc, x, 1 - h, i, r, edge)
            if i % 2 == 0:
                forward(cc, x, 1 - h, i, par, c)
            wait_recv(*chunk(away, h, i))
            if i % 2 == 1:
                forward(cc, away, h, i, r, other)
            to_sib(cc, x, 1 - h, i)
            to_sib(cc, away, h, i)
        for i in [*range(0, parts, 2), *range(1, parts, 2)]:
            wait_recv(*chunk(away, 1 - h, i))
            if i % 2 == 0:
                forward(cc, away, 1 - h, i, r, edge)
            to_sib(cc, away, 1 - h, i)

    def edge_gather(cc, *_):
        h = cc // 2
        for i in range(parts):
            wait_recv(*chunk(x, h, i))
            forward(cc, x, h, i, par, c)
            to_sib(cc, x, h, i)
        for i in range(parts):
            wait_recv(*chunk(x, 1 - h, i))
            if i % 2 == 1:
                forward(cc, x, 1 - h, i, par, c)
            to_sib(cc, x, 1 - h, i)
            wait_recv(*chunk(away, h, i))
            to_sib(cc, away, h, i)
        for i in range(parts):
            wait_recv(*chunk(away, 1 - h, i))
            to_sib(cc, away, 1 - h, i)

    at_each_col(hub_gather, edge_gather)
    for s in range(supers):
        for h in range(2):
            for i in range(parts):
                wait_recv(res.at[s, 1 - k, rows_at(h, i), :], s_sib.at[(s * 2 + h) * parts + i])

    wait_sends()

    @pl.when(is_hub)
    def _():
        for h in range(nb):
            copy_to(vpart.at[:, v_cols(h)], vrecv.at[:, v_cols(h)], s_v.at[h], sib, c, v_slot + h).wait_send()

    for rr in range(n_r):
        @pl.when((r == rr) & sends_d)
        def _():
            copy_to(d_src(rr, away), d_slice(rr), s_d.at[rr], par, c, 0).wait_send()

        @pl.when((r == rr) & is_hub)
        def _():
            copy_to(d_src(rr, x), d_slice(rr), s_d.at[rr], sib, c, 1).wait_send()

        @pl.when((rr == par) & is_hub)
        def _():
            copy_to(d_slice(rr), d_slice(rr), s_d.at[rr], sib, c, 2).wait_send()

        @pl.when((rr == par) & is_edge & (k == 1))
        def _():
            copy_to(d_slice(rr), d_slice(rr), s_d.at[rr], r, hub, 3).wait_send()


def unpack_kernel(supers, nb, off_in, res, off_out, diag_out, stage, sems):
    copies = [pltpu.make_async_copy(off_in, off_out, sems.at[supers * nb])]
    copies[0].start()
    place = {pair: (core, b) for core, some in enumerate(pairs_of(nb)) for b, pair in enumerate(some)}
    for s in range(supers):
        for i in range(nb):
            for j in range(nb):
                core, b = place[max(i, j), min(i, j)]
                v = res[s, core, b * LANES : (b + 1) * LANES, :]
                stage[s, i * LANES : (i + 1) * LANES, j * LANES : (j + 1) * LANES] = v if i >= j else jnp.transpose(v)
            at = (s, pl.ds(i * LANES, LANES))
            copies.append(pltpu.make_async_copy(stage.at[at], diag_out.at[at], sems.at[s * nb + i]))
            copies[-1].start()
    for cp in copies:
        cp.wait()


def fused_body(sigma_anc, anc_factor, diag_inverse, pattern):
    rows_dev, supers, width = anc_factor.shape
    n_r = lax.axis_size("row")
    n_c = lax.axis_size("col")
    total_rows = rows_dev * n_r * n_c
    nb = width // LANES
    packed = len(pairs_of(nb)[0]) * LANES
    q = packed // (2 * PARTS)
    slots = len(columns_of(nb)[0])
    f32 = lambda *shape: pltpu.VMEM(shape, jnp.float32)
    dma = lambda n: pltpu.SemaphoreType.DMA((n,))
    vm = pl.BlockSpec(memory_space=pltpu.VMEM)
    linear = jnp.transpose(anc_factor.reshape(rows_dev, supers, nb, LANES), (0, 2, 1, 3))
    linear = linear.reshape(rows_dev * nb * supers, LANES)
    hbm = pl.BlockSpec(memory_space=pl.ANY)
    off, res = pl.pallas_call(
        functools.partial(fused_kernel, n_r, n_c, supers, width, rows_dev, total_rows // pattern.shape[1], PARTS),
        out_shape=(
            pltpu.VMEM((rows_dev * supers * nb, LANES), jnp.float32),
            pltpu.VMEM((supers, 2, packed, LANES), jnp.float32),
        ),
        in_specs=[hbm, hbm, hbm, pl.BlockSpec(memory_space=pltpu.SMEM)],
        out_specs=(vm, vm),
        scratch_shapes=[
            f32(*sigma_anc.shape),
            f32(*linear.shape),
            f32(supers, rows_dev, width),
            f32(n_r * rows_dev, n_c * rows_dev),
            f32(2, n_c, rows_dev, width),
            f32(2, n_c, 2 * rows_dev, n_c * rows_dev),
            f32(width, width),
            f32(n_r, 2 * rows_dev, width),
            f32(2 * n_r * rows_dev, width),
            f32(2 * n_r * rows_dev, width),
            f32(slots, n_r, 2, rows_dev, LANES),
            f32(n_r, slots, rows_dev, LANES),
            f32(packed, LANES),
            f32(PARTS, q, LANES),
            dma(64 + 16 * PARTS),
            dma(2 * n_c), dma(2 * n_c), dma(n_r), dma(2), dma(nb), dma(n_r), dma(PARTS),
            dma(2 * supers * PARTS), dma(2 * supers * PARTS), dma(4),
        ],
        compiler_params=pltpu.CompilerParams(
            collective_id=0, has_side_effects=True, vmem_limit_bytes=58 * 1024 * 1024
        ),
    )(sigma_anc, linear, diag_inverse, pattern)
    off, diag = pl.pallas_call(
        functools.partial(unpack_kernel, supers, nb),
        out_shape=(
            jax.ShapeDtypeStruct(off.shape, jnp.float32),
            jax.ShapeDtypeStruct((supers, width, width), jnp.float32),
        ),
        in_specs=[vm, vm],
        out_specs=(hbm, hbm),
        scratch_shapes=[f32(supers, width, width), dma(supers * nb + 1)],
        compiler_params=pltpu.CompilerParams(vmem_limit_bytes=8 * 1024 * 1024),
    )(off, res)
    off = jnp.transpose(off.reshape(rows_dev, nb, supers, LANES), (0, 2, 1, 3))
    return off.reshape(anc_factor.shape), diag


def fits(sigma_anc, anc_factor, diag_inverse):
    rows_dev, supers, width = anc_factor.shape
    n_r = lax.axis_size("row")
    n_c = lax.axis_size("col")
    nb = width // LANES
    return (
        n_r == n_c
        and n_r == 2 * supers
        and supers == 2
        and sigma_anc.shape[0] == sigma_anc.shape[1]
        and diag_inverse.shape[2] % LANES == 0
        and nb % 4 == 0
        and rows_dev % SUBLANES == 0
        and width % (n_c * SUBLANES) == 0
        and len(pairs_of(nb)[0]) == len(pairs_of(nb)[1])
        and (len(pairs_of(nb)[0]) * LANES) % (2 * PARTS * SUBLANES) == 0
    )


def plain_body(sigma_anc, anc_factor, diag_inverse, pattern):
    precise = lax.Precision.HIGHEST
    rows_dev, supers, super_width = anc_factor.shape
    row_count = lax.axis_size("row")
    col_count = lax.axis_size("col")
    position = lax.axis_index("row") * col_count + lax.axis_index("col")
    total_rows = rows_dev * row_count * col_count
    block_size = total_rows // pattern.shape[1]
    flat_mask = jnp.repeat(pattern.astype(jnp.float32), block_size, axis=1)
    own_mask = jnp.transpose(lax.dynamic_slice_in_dim(flat_mask, position * rows_dev, rows_dev, 1))[
        :, :, None
    ]
    device_total = row_count * col_count
    share = -(-super_width // device_total)
    masked_factor = anc_factor * own_mask
    flattened = masked_factor.reshape(rows_dev, -1)
    gathered = lax.all_gather(flattened, "row", axis=0, tiled=True)
    stacked = gathered.reshape(row_count, rows_dev, flattened.shape[1])
    turned = lax.all_to_all(stacked, "col", split_axis=0, concat_axis=1, tiled=True)
    column_block = turned.reshape(row_count * rows_dev, flattened.shape[1])
    summed_rows = lax.psum_scatter(
        jnp.dot(sigma_anc, column_block, precision=precise, preferred_element_type=jnp.float32),
        "col",
        scatter_dimension=0,
        tiled=True,
    )
    off_factor = -(summed_rows.reshape(masked_factor.shape) * own_mask)
    both_rows = jnp.concatenate([masked_factor, off_factor], axis=0)
    column_piece = lax.all_gather(diag_inverse, "row", axis=2, tiled=True)
    product = jnp.einsum("rsk,skj->rsj", both_rows, column_piece, precision=precise)
    own_rows = lax.dynamic_slice_in_dim(column_piece, position * share, share, 1)
    scaled = product[:rows_dev]
    sel_off = product[rows_dev:]
    diag_term = jnp.einsum("skj,skl->sjl", own_rows, own_rows, precision=precise)
    partial_value = diag_term - jnp.einsum("rsj,rsl->sjl", scaled, sel_off, precision=precise)
    sel_diag = lax.psum(partial_value, ("row", "col"))
    return (sel_off, sel_diag)


def body(sigma_anc, anc_factor, diag_inverse, pattern):
    run = fused_body if fits(sigma_anc, anc_factor, diag_inverse) else plain_body
    return run(sigma_anc, anc_factor, diag_inverse, pattern)


def solution(mesh):
    return jax.shard_map(
        body,
        mesh=mesh,
        in_specs=(
            P(("grp", "row"), "col"),
            P(("grp", "row", "col"), None, None),
            P("grp", None, "row"),
            P(),
        ),
        out_specs=(P(("grp", "row", "col"), None, None), P("grp", None, None)),
        check_vma=False,
    )
```

time: 60.2 us -> 46.6 us (0.77)
  Pallas kernels: 55.7 us -> 45.7 us
  local copies, waits for them, and re-layouts: 3.57 us -> 0 us
    pallas_call x1, Pallas kernels: 54.2 us -> 44.2 us  [fused_body(): pl.pallas_call(functools.partial(fused_kernel, n_r, n_c, supers, width, r...]
    unnamed x8 -> x0, local copies, waits for them, and re-layouts: 3.57 us -> none
where the time goes in v4:
time: 46.6 us; the launch traced here: 46.3 us
  Pallas kernels  45.7 us (98%)
  between operations  0.64 us (1%)
    pallas_call x1, Pallas kernels, fused_body(): pl.pallas_call(functools.partial(fused_kernel, n_r, n_c, supers, width, r...  44.2 us
    pallas_call x1, Pallas kernels, fused_body(): pl.pallas_call(functools.partial(unpack_kernel, supers, nb), out_shape=(j...  1.52 us

profile of v4, /device:TPU:0, one launch (start us, length us, event | category | flops | bytes accessed | tf_op | source)
XLA Modules:
  0.0 46.3 jit_solution(2718309240429429126)
XLA Ops:
  0.6 44.2 %shard_map.59 = (f32[384,128]{1,0:T(8,128)S(1)}, f32[2,2,640,128]{3,2,1,0:T(8,128)S(1)}) custom-call(f32[192,192]{1,0:T(8,128)} %sig_hbm.1, f32[384,128]{1,0:T(8,128)} %bitcast.10, f32[2,512,128]{2,1,0:T(8,128)} %d_ref.1, s32[2,6]{1,0:T(2,128)} %pat_ref.1), custom_call_target="tpu_custom_call" | custom-call | tf_op jit(solution)/shard_map/pallas_call | solution.py:444
  44.8 1.5 %shard_map.60 = (f32[384,128]{1,0:T(8,128)}, f32[2,512,512]{2,1,0:T(8,128)}) custom-call(f32[384,128]{1,0:T(8,128)S(1)} %get-tuple-element.6.off_in, f32[2,2,640,128]{3,2,1,0:T(8,128)S(1)} %get-tuple-element.7.res), custom_call_target="tpu_custom_call" | custom-call | tf_op jit(solution)/shard_map/pallas_call | solution.py:475

commit v5 on v4

--- a/solution.py
+++ b/solution.py
@@ -1,4 +1,5 @@
 import functools
+import math
 
 import jax
 import jax.numpy as jnp
@@ -40,10 +41,10 @@
 
 def fused_kernel(
     n_r, n_c, supers, width, rows_dev, block_size, parts,
-    sig_hbm, a_hbm, d_ref, pat_ref,
-    off_ref, res,
-    sig_ref, a_ref, av, sig_t, wz, sq, dfull, scl, vpart, vrecv, of, offr, gpart, grecv,
-    send_sems, s_w, s_sq, s_d, s_scl, s_v, s_off, s_h, s_g, s_sib, local_sems,
+    sig_hbm, a_hbm, d_ref, pat_hbm,
+    off_out, res,
+    pat_ref, sig_ref, a_ref, av, sig_t, wz, sq, dfull, scl, vpart, vrecv, of, offr, gpart, grecv, mine, off_ref, spare,
+    send_sems, s_w, s_sq, s_d, s_scl, s_v, s_off, s_h, s_g, s_sib, s_mine, local_sems,
 ):
     r = lax.axis_index("row")
     c = lax.axis_index("col")
@@ -66,10 +67,10 @@
     hub = low + side
     is_hub = hub == c
     is_edge = hub != c
-    plans = [[] for _ in range(n_c)]
-    done = [0] * n_c
-    v_slot = 4
-    z_slot = v_slot + nb
+    single = [[] for _ in range(n_c)]
+    bulk = [[0, 0] for _ in range(n_c)]
+    late = [0]
+    bulk_slot, v_slot, single_slot = 4, 6, 7
 
     def copy_to(src, dst, rsem, row, col, slot):
         return pltpu.make_async_remote_copy(
@@ -85,16 +86,22 @@
                 pl.when(c == cc)(functools.partial(part, cc, n_c - 1 - cc))
 
     def post(cc, refs, row, col):
-        slot = z_slot + len(plans[cc])
+        bulk[cc][late[0]] += math.prod(refs()[0].shape)
+        copy_to(*refs(), row, col, bulk_slot + late[0]).start()
+
+    def post_single(cc, refs, row, col):
+        slot = single_slot + len(single[cc])
         make = lambda: copy_to(*refs(), row, col, slot)
         make().start()
-        plans[cc].append(make)
-
-    def wait_sends():
+        single[cc].append(make)
+
+    def wait_sends(part):
         def at(cc, *_):
-            for make in plans[cc][done[cc] :]:
-                make().wait_send()
-            done[cc] = len(plans[cc])
+            whole = spare.at[pl.ds(0, bulk[cc][part] // LANES), :]
+            pltpu.make_async_copy(whole, whole, send_sems.at[bulk_slot + part]).wait()
+            if part == 0:
+                for make in single[cc]:
+                    make().wait_send()
 
         at_each_col(at, at)
 
@@ -104,6 +111,7 @@
     loads = [
         pltpu.make_async_copy(a_hbm, a_ref, local_sems.at[2]),
         pltpu.make_async_copy(sig_hbm, sig_ref, local_sems.at[3]),
+        pltpu.make_async_copy(pat_hbm, pat_ref, local_sems.at[1]),
     ]
     for cp in loads:
         cp.start()
@@ -125,6 +133,7 @@
             m = jnp.where(inside, pat_ref[s, b].astype(jnp.float32), m)
         return m
 
+    loads[2].wait()
     loads[0].wait()
     for s in range(supers):
         mask = mask_of((r * n_c + c) * rows_dev, rows_dev, s)
@@ -137,7 +146,7 @@
     pl.semaphore_wait(barrier, n_c + 5)
 
     rows_w = lambda own, j: (wz.at[own, j], s_w.at[own * n_c + j])
-    rows_s = lambda own, j: (sq.at[own, j], s_sq.at[own * n_c + j])
+    rows_s = lambda own, j: (sq.at[own, j], s_sq.at[n_c if own else j])
     half_of = lambda h: sig_t.at[pl.ds(h * side_rows, side_rows), :]
     d_slice = lambda rr: dfull.at[pl.ds(rr * piece, width - rr * piece), pl.ds(rr * piece, piece)]
     d_src = lambda rr, s: d_ref.at[s, pl.ds(rr * piece, width - rr * piece), :]
@@ -145,16 +154,16 @@
 
     def hub_first(cc, other):
         post(cc, lambda: (av.at[away], *rows_w(1, cc)), par, c)
-        post(cc, lambda: (half_of(1 - cc // 2), *rows_s(0, cc)), r, other)
+        post_single(cc, lambda: (half_of(1 - cc // 2), *rows_s(0, cc)), r, other)
         post(cc, lambda: (av.at[x], *rows_w(0, cc)), r, other)
-        post(cc, lambda: (half_of(cc // 2), *rows_s(1, cc)), par, c)
+        post_single(cc, lambda: (half_of(cc // 2), *rows_s(1, cc)), par, c)
 
     def edge_first(cc, other):
         near = low + cc // 2
         post(cc, lambda: (av.at[away], *rows_w(1, cc)), par, c)
         post(cc, lambda: (av.at[x], *rows_w(0, cc)), r, near)
-        post(cc, lambda: (half_of(1 - cc // 2), *rows_s(0, cc)), r, n_c - 1 - near)
-        post(cc, lambda: (half_of(cc // 2), *rows_s(0, cc)), r, near)
+        post_single(cc, lambda: (half_of(1 - cc // 2), *rows_s(0, cc)), r, n_c - 1 - near)
+        post_single(cc, lambda: (half_of(cc // 2), *rows_s(0, cc)), r, near)
 
     at_each_col(hub_first, edge_first)
     for rr in range(n_r):
@@ -182,7 +191,7 @@
         post(cc, lambda: (wz.at[0, edge], *rows_w(0, edge)), r, other)
         for j in (other, edge, n_c - 1 - edge):
             wait_recv(*rows_s(0, j))
-            post(cc, lambda j=j: (sq.at[0, j], *rows_s(1, j)), par, c)
+            post_single(cc, lambda j=j: (sq.at[0, j], *rows_s(1, j)), par, c)
 
     def hub_pass_last(cc, other):
         edge = 0 if cc == low else n_c - 1
@@ -240,7 +249,7 @@
 
     def hub_scl(cc, *_):
         post(cc, lambda: (scl.at[r], scl.at[r], s_scl.at[0]), sib, c)
-        post(cc, lambda: (scl.at[par], scl.at[par], s_scl.at[1]), sib, c)
+        post(cc, lambda: (scl.at[par], scl.at[par], s_scl.at[0]), sib, c)
 
     at_each_col(hub_scl)
 
@@ -262,8 +271,7 @@
         for j in (other, n_c - 1 - edge):
             wait_recv(*rows_w(own, j))
         if own == 1:
-            for j in range(n_c):
-                wait_recv(*rows_s(1, j))
+            wait_recv(sq.at[1], s_sq.at[n_c])
 
     at_each_col(functools.partial(hub_wait, 0))
 
@@ -279,13 +287,11 @@
         sigma, ws = v_of(1)
         for h in range(nb):
             vpart[:, v_cols(h)] = vpart[:, v_cols(h)] + dot3(sigma, cut(ws, h))
-            copy_to(vpart.at[:, v_cols(h)], vrecv.at[:, v_cols(h)], s_v.at[h], sib, c, v_slot + h).start()
-
-        wait_recv(scl.at[sib], s_scl.at[0])
-        wait_recv(scl.at[dia], s_scl.at[1])
+            copy_to(vpart.at[:, v_cols(h)], vrecv.at[:, v_cols(h)], s_v.at[0], sib, c, v_slot).start()
+
+        wait_recv(scl.at[pl.ds(0, 2)], s_scl.at[0])
         all_scl = split(scl[...].reshape(n_r * side_rows, width))
-        for h in range(nb):
-            wait_recv(vrecv.at[:, v_cols(h)], s_v.at[h])
+        wait_recv(vrecv, s_v.at[0])
         vs = split((vpart[...] + vrecv[...]) * mask_rows())
         for core in range(2):
             @pl.when(k == core)
@@ -309,38 +315,41 @@
             post(cc, lambda i=i: (gpart.at[rows_at(1 - cc // 2, i), :], grecv.at[i], s_h.at[i]), r, other)
         edge = 0 if cc == low else n_c - 1
         for row in (sib, par, dia):
-            post(cc, lambda row=row: (of.at[:, row, cc - 2 * (cc // 2)], offr.at[r], s_off.at[r]), row, cc)
+            post(cc, lambda row=row: (of.at[:, row, cc - 2 * (cc // 2)], offr.at[r], s_off.at[0]), row, cc)
         for row in (r, sib, par, dia):
-            post(cc, lambda row=row: (of.at[:, row, edge - 2 * (cc // 2)], offr.at[r], s_off.at[r]), row, edge)
-        pltpu.make_async_copy(of.at[:, r, cc - 2 * (cc // 2)], offr.at[r], s_off.at[r]).start()
+            post(cc, lambda row=row: (of.at[:, row, edge - 2 * (cc // 2)], offr.at[r], s_off.at[0]), row, edge)
+        pltpu.make_async_copy(of.at[:, r, cc - 2 * (cc // 2)], offr.at[r], s_off.at[0]).start()
 
     at_each_col(hub_scatter)
-    wait_sends()
+    late[0] = 1
 
     def forward(cc, s, h, i, row, col):
         post(cc, lambda: (held(s, h, i), *chunk(s, h, i)), row, col)
 
     def to_sib(cc, s, h, i):
-        post(cc, lambda: (held(s, h, i), held(s, h, i), s_sib.at[(s * 2 + h) * parts + i]), sib, c)
+        post(cc, lambda: (held(s, h, i), held(s, h, i), s_sib.at[0]), sib, c)
 
     def hub_reduce(cc, other):
         h = cc // 2
         edge = 0 if cc == low else n_c - 1
         for i in range(parts):
             wait_recv(grecv.at[i], s_h.at[i])
-            res[x, k, rows_at(h, i), :] = gpart[rows_at(h, i), :] + grecv[i]
-            forward(cc, x, h, i, par, c)
-            forward(cc, x, h, i, r, other)
-            forward(cc, x, h, i, r, edge)
-            to_sib(cc, x, h, i)
+            mine[i] = gpart[rows_at(h, i), :] + grecv[i]
+            pltpu.make_async_copy(mine.at[i], held(x, h, i), s_mine.at[0]).start()
+            for row, col in ((par, c), (r, other), (r, edge)):
+                post(cc, lambda i=i: (mine.at[i], *chunk(x, h, i)), row, col)
+            post(cc, lambda i=i: (mine.at[i], held(x, h, i), s_sib.at[0]), sib, c)
 
     at_each_col(hub_reduce)
 
+    wait_recv(offr, s_off.at[0])
     for row in range(n_r):
-        wait_recv(offr.at[row], s_off.at[row])
         for slot, t in enumerate(columns[row % 2]):
             at = pl.ds(t * supers + row // 2, rows_dev, stride=nb * supers)
             off_ref[at, :] = -offr[row, slot]
+    off_copy = pltpu.make_async_copy(off_ref, off_out, local_sems.at[2])
+    off_copy.start()
+    wait_sends(0)
 
     def hub_gather(cc, other):
         h = cc // 2
@@ -379,17 +388,18 @@
             to_sib(cc, away, 1 - h, i)
 
     at_each_col(hub_gather, edge_gather)
-    for s in range(supers):
-        for h in range(2):
-            for i in range(parts):
-                wait_recv(res.at[s, 1 - k, rows_at(h, i), :], s_sib.at[(s * 2 + h) * parts + i])
-
-    wait_sends()
-
-    @pl.when(is_hub)
-    def _():
-        for h in range(nb):
-            copy_to(vpart.at[:, v_cols(h)], vrecv.at[:, v_cols(h)], s_v.at[h], sib, c, v_slot + h).wait_send()
+    theirs = res.at[:, 1 - k]
+    wait_recv(theirs, s_sib.at[0])
+    @pl.when(is_hub)
+    def _():
+        pltpu.make_async_copy(mine, mine, s_mine.at[0]).wait()
+
+    off_copy.wait()
+    wait_sends(1)
+
+    @pl.when(is_hub)
+    def _():
+        copy_to(vpart, vrecv, s_v.at[0], sib, c, v_slot).wait_send()
 
     for rr in range(n_r):
         @pl.when((r == rr) & sends_d)
@@ -447,9 +457,10 @@
             pltpu.VMEM((rows_dev * supers * nb, LANES), jnp.float32),
             pltpu.VMEM((supers, 2, packed, LANES), jnp.float32),
         ),
-        in_specs=[hbm, hbm, hbm, pl.BlockSpec(memory_space=pltpu.SMEM)],
-        out_specs=(vm, vm),
+        in_specs=[hbm, hbm, hbm, hbm],
+        out_specs=(hbm, hbm),
         scratch_shapes=[
+            pltpu.SMEM(pattern.shape, jnp.int32),
             f32(*sigma_anc.shape),
             f32(*linear.shape),
             f32(supers, rows_dev, width),
@@ -464,9 +475,12 @@
             f32(n_r, slots, rows_dev, LANES),
             f32(packed, LANES),
             f32(PARTS, q, LANES),
-            dma(64 + 16 * PARTS),
-            dma(2 * n_c), dma(2 * n_c), dma(n_r), dma(2), dma(nb), dma(n_r), dma(PARTS),
-            dma(2 * supers * PARTS), dma(2 * supers * PARTS), dma(4),
+            f32(PARTS, q, LANES),
+            f32(*linear.shape),
+            f32(8 * packed + 8 * n_r * rows_dev * nb, LANES),
+            dma(7 + n_c + 1),
+            dma(2 * n_c), dma(n_c + 1), dma(n_r), dma(1), dma(1), dma(1), dma(PARTS),
+            dma(2 * supers * PARTS), dma(1), dma(1), dma(4),
         ],
         compiler_params=pltpu.CompilerParams(
             collective_id=0, has_side_effects=True, vmem_limit_bytes=58 * 1024 * 1024

time: 46.6 us -> 43.8 us (0.940)
  Pallas kernels: 45.7 us -> 43 us
    pallas_call x1, Pallas kernels: 44.2 us -> 41.5 us  [fused_body(): pl.pallas_call(functools.partial(fused_kernel, n_r, n_c, supers, width, r...]
where the time goes in v5:
time: 43.8 us; the launch traced here: 43.7 us
  Pallas kernels  43 us (98%)
  between operations  0.64 us (1%)
    pallas_call x1, Pallas kernels, fused_body(): pl.pallas_call(functools.partial(fused_kernel, n_r, n_c, supers, width, r...  41.5 us
    pallas_call x1, Pallas kernels, fused_body(): pl.pallas_call(functools.partial(unpack_kernel, supers, nb), out_shape=(j...  1.52 us

profile of v5, /device:TPU:0, one launch (start us, length us, event | category | flops | bytes accessed | tf_op | source)
XLA Modules:
  0.0 43.7 jit_solution(5089734388222676633)
XLA Ops:
  0.6 41.5 %shard_map.59 = (f32[384,128]{1,0:T(8,128)S(1)}, f32[2,2,640,128]{3,2,1,0:T(8,128)S(1)}) custom-call(f32[192,192]{1,0:T(8,128)} %sig_hbm.1, f32[384,128]{1,0:T(8,128)} %bitcast.10, f32[2,512,128]{2,1,0:T(8,128)} %d_ref.1, s32[2,6]{1,0:T(2,128)} %pat_hbm.1), custom_call_target="tpu_custom_call" | custom-call | tf_op jit(solution)/shard_map/pallas_call | solution.py:454
  42.1 1.5 %shard_map.60 = (f32[384,128]{1,0:T(8,128)}, f32[2,512,512]{2,1,0:T(8,128)}) custom-call(f32[384,128]{1,0:T(8,128)S(1)} %get-tuple-element.6.off_in, f32[2,2,640,128]{3,2,1,0:T(8,128)S(1)} %get-tuple-element.7.res), custom_call_target="tpu_custom_call" | custom-call | tf_op jit(solution)/shard_map/pallas_call | solution.py:489

commit v6 on v5

--- a/solution.py
+++ b/solution.py
@@ -70,6 +70,7 @@
     single = [[] for _ in range(n_c)]
     bulk = [[0, 0] for _ in range(n_c)]
     late = [0]
+    direct = parts // 2
     bulk_slot, v_slot, single_slot = 4, 6, 7
 
     def copy_to(src, dst, rsem, row, col, slot):
@@ -88,6 +89,15 @@
     def post(cc, refs, row, col):
         bulk[cc][late[0]] += math.prod(refs()[0].shape)
         copy_to(*refs(), row, col, bulk_slot + late[0]).start()
+
+    def post_hub(core, refs, row, col):
+        if core == 0:
+            for cc in (low, low + 1):
+                bulk[cc][late[0]] += math.prod(refs()[0].shape)
+        copy_to(*refs(), row, col, bulk_slot + late[0]).start()
+
+    def off_refs(row, col, kind):
+        return lambda: (of.at[:, row, col - 2 * side], offr.at[r], s_off.at[kind])
 
     def post_single(cc, refs, row, col):
         slot = single_slot + len(single[cc])
@@ -147,6 +157,8 @@
 
     rows_w = lambda own, j: (wz.at[own, j], s_w.at[own * n_c + j])
     rows_s = lambda own, j: (sq.at[own, j], s_sq.at[n_c if own else j])
+    half_rows = rows_dev // 2
+    rows_h = lambda j, i: (wz.at[1, j, pl.ds(i * half_rows, half_rows), :], s_w.at[(1 + i) * n_c + j])
     half_of = lambda h: sig_t.at[pl.ds(h * side_rows, side_rows), :]
     d_slice = lambda rr: dfull.at[pl.ds(rr * piece, width - rr * piece), pl.ds(rr * piece, piece)]
     d_src = lambda rr, s: d_ref.at[s, pl.ds(rr * piece, width - rr * piece), :]
@@ -163,7 +175,6 @@
         post(cc, lambda: (av.at[away], *rows_w(1, cc)), par, c)
         post(cc, lambda: (av.at[x], *rows_w(0, cc)), r, near)
         post_single(cc, lambda: (half_of(1 - cc // 2), *rows_s(0, cc)), r, n_c - 1 - near)
-        post_single(cc, lambda: (half_of(cc // 2), *rows_s(0, cc)), r, near)
 
     at_each_col(hub_first, edge_first)
     for rr in range(n_r):
@@ -189,20 +200,26 @@
         post(cc, lambda: (wz.at[1, cc], *rows_w(1, cc)), r, other)
         wait_recv(*rows_w(0, edge))
         post(cc, lambda: (wz.at[0, edge], *rows_w(0, edge)), r, other)
-        for j in (other, edge, n_c - 1 - edge):
+        for j in (other, n_c - 1 - edge):
             wait_recv(*rows_s(0, j))
             post_single(cc, lambda j=j: (sq.at[0, j], *rows_s(1, j)), par, c)
 
     def hub_pass_last(cc, other):
         edge = 0 if cc == low else n_c - 1
-        wait_recv(*rows_w(1, edge))
-        post(cc, lambda: (wz.at[1, edge], *rows_w(1, edge)), r, other)
+        for i in range(2):
+            wait_recv(*rows_h(edge, i))
+            post(cc, lambda i=i: (rows_h(edge, i)[0], *rows_h(edge, i)), r, other)
+        wait_recv(*rows_s(0, edge))
+        post_single(cc, lambda: (sq.at[0, edge], *rows_s(1, edge)), par, c)
 
     def edge_pass(cc, other):
         wait_recv(*rows_w(1, cc))
-        post(cc, lambda: (wz.at[1, cc], *rows_w(1, cc)), r, low + cc // 2)
+        for i in range(2):
+            post(cc, lambda i=i: (rows_h(cc, i)[0], *rows_h(cc, i)), r, low + cc // 2)
+        post_single(cc, lambda: (half_of(cc // 2), *rows_s(0, cc)), r, low + cc // 2)
 
     at_each_col(hub_pass, edge_pass)
+    at_each_col(hub_pass_last)
     for rr in range(n_r):
         @pl.when((rr == par) & is_hub)
         def _():
@@ -215,12 +232,32 @@
         def _():
             wait_recv(d_slice(rr), s_d.at[rr])
             copy_to(d_slice(rr), d_slice(rr), s_d.at[rr], r, hub, 3).start()
-    at_each_col(hub_pass_last)
     for rr in range(n_r):
         @pl.when((rr == par) & is_hub & (k == 1))
         def _():
             wait_recv(d_slice(rr), s_d.at[rr])
             copy_to(d_slice(rr), d_slice(rr), s_d.at[rr], sib, c, 2).start()
+    def v_of(own):
+        sigma = split(sq[own].reshape(n_r * side_rows, block_rows))
+        return sigma, split(wz[own].reshape(block_rows, width))
+
+    def hub_wait(own, cc, other):
+        edge = 0 if cc == low else n_c - 1
+        wait_recv(*rows_w(own, other))
+        for i in range(2):
+            if own == 1:
+                wait_recv(*rows_h(n_c - 1 - edge, i))
+            elif i == 0:
+                wait_recv(*rows_w(0, n_c - 1 - edge))
+        if own == 1:
+            wait_recv(sq.at[1], s_sq.at[n_c])
+
+    at_each_col(functools.partial(hub_wait, 0))
+
+    @pl.when(is_hub)
+    def _():
+        vpart[...] = dot3(*v_of(0))
+
     for rr in range(n_r):
         @pl.when(((rr == sib) | (rr == dia)) & is_hub)
         def _():
@@ -230,6 +267,7 @@
         def _():
             pltpu.make_async_copy(d_src(rr, x), d_slice(rr), local_sems.at[0]).wait()
 
+    rows_at = lambda h, i: pl.ds((h * parts + i) * q, q)
     over_rows = ((0,), (0,))
     lanes = lambda j: slice(j * LANES, (j + 1) * LANES)
     cut = lambda pair, j: (pair[0][:, lanes(j)], pair[1][:, lanes(j)])
@@ -262,24 +300,28 @@
                 for b, (i, j) in enumerate(pairs[core]):
                     gpart[lanes(b), :] = dot3(cut(dz, i), cut(dz, j), over_rows)
 
-    def v_of(own):
-        sigma = split(sq[own].reshape(n_r * side_rows, block_rows))
-        return sigma, split(wz[own].reshape(block_rows, width))
-
-    def hub_wait(own, cc, other):
-        edge = 0 if cc == low else n_c - 1
-        for j in (other, n_c - 1 - edge):
-            wait_recv(*rows_w(own, j))
-        if own == 1:
-            wait_recv(sq.at[1], s_sq.at[n_c])
-
-    at_each_col(functools.partial(hub_wait, 0))
-
-    @pl.when(is_hub)
-    def _():
-        vpart[...] = dot3(*v_of(0))
-
     at_each_col(functools.partial(hub_wait, 1))
+    far = n_c - 1 - c
+
+    def sum_pairs(core, own_side, all_scl, ofs):
+        first = (1 - own_side) * parts * q
+        order = sorted(range(len(pairs[core])), key=lambda b: ((b + 1) * LANES <= first, b))
+        left_parts = list(range(parts))
+        ready = set()
+        for b in order:
+            i, j = pairs[core][b]
+            left, right = (cut(all_scl, i), ofs[j]) if j in ofs else (ofs[i], cut(all_scl, j))
+            gpart[lanes(b), :] += dot3(left, right, over_rows)
+            ready.add(b)
+            for part in list(left_parts):
+                at = first + part * q
+                if set(range(at // LANES, (at + q - 1) // LANES + 1)) <= ready:
+                    left_parts.remove(part)
+                    refs = lambda part=part: (gpart.at[rows_at(1 - own_side, part), :], grecv.at[part], s_h.at[part])
+                    if core == 0:
+                        bulk[low + own_side][0] += math.prod(refs()[0].shape)
+                    copy_to(*refs(), r, far, bulk_slot).start()
+
     v_cols = lambda h: slice(h * LANES, (h + 1) * LANES)
 
     @pl.when(is_hub)
@@ -302,25 +344,15 @@
                     v = dot3((vs[0][:, at:], vs[1][:, at:]), split(dfull[at:, at : at + LANES]))
                     of[slot] = v.reshape(n_r, 2, rows_dev, LANES)
                     ofs[j] = split(v)
-                for b, (i, j) in enumerate(pairs[core]):
-                    left, right = (cut(all_scl, i), ofs[j]) if j in ofs else (ofs[i], cut(all_scl, j))
-                    gpart[lanes(b), :] += dot3(left, right, over_rows)
-
-    rows_at = lambda h, i: pl.ds((h * parts + i) * q, q)
+                for row, col, kind in ((par, c, 1), (dia, c, 1), (r, mate, 0), (sib, mate, 0), (sib, c, 0), (par, mate, 1), (dia, mate, 1)):
+                    post_hub(core, off_refs(row, c if col is c else mate, kind), row, col)
+                pltpu.make_async_copy(*off_refs(r, c, 0)()).start()
+                for own_side in range(2):
+                    pl.when(side == own_side)(functools.partial(sum_pairs, core, own_side, all_scl, ofs))
+
     chunk = lambda s, h, i: (res.at[s, k, rows_at(h, i), :], s_g.at[(s * 2 + h) * parts + i])
     held = lambda s, h, i: res.at[s, k, rows_at(h, i), :]
 
-    def hub_scatter(cc, other):
-        for i in range(parts):
-            post(cc, lambda i=i: (gpart.at[rows_at(1 - cc // 2, i), :], grecv.at[i], s_h.at[i]), r, other)
-        edge = 0 if cc == low else n_c - 1
-        for row in (sib, par, dia):
-            post(cc, lambda row=row: (of.at[:, row, cc - 2 * (cc // 2)], offr.at[r], s_off.at[0]), row, cc)
-        for row in (r, sib, par, dia):
-            post(cc, lambda row=row: (of.at[:, row, edge - 2 * (cc // 2)], offr.at[r], s_off.at[0]), row, edge)
-        pltpu.make_async_copy(of.at[:, r, cc - 2 * (cc // 2)], offr.at[r], s_off.at[0]).start()
-
-    at_each_col(hub_scatter)
     late[0] = 1
 
     def forward(cc, s, h, i, row, col):
@@ -342,13 +374,25 @@
 
     at_each_col(hub_reduce)
 
-    wait_recv(offr, s_off.at[0])
-    for row in range(n_r):
-        for slot, t in enumerate(columns[row % 2]):
-            at = pl.ds(t * supers + row // 2, rows_dev, stride=nb * supers)
-            off_ref[at, :] = -offr[row, slot]
-    off_copy = pltpu.make_async_copy(off_ref, off_out, local_sems.at[2])
-    off_copy.start()
+    def put_off(own):
+        first = x if own else away
+        wait_recv(offr.at[pl.ds(2 * first, 2)], s_off.at[0 if own else 1])
+        for s in range(supers):
+            @pl.when(first == s)
+            def _():
+                for row in (2 * s, 2 * s + 1):
+                    for slot, t in enumerate(columns[row % 2]):
+                        at = pl.ds(t * supers + s, rows_dev, stride=nb * supers)
+                        off_ref[at, :] = -offr[row, slot]
+
+    off_copy = lambda: pltpu.make_async_copy(off_ref, off_out, local_sems.at[2])
+    put_off(True)
+
+    @pl.when(is_hub)
+    def _():
+        put_off(False)
+        off_copy().start()
+
     wait_sends(0)
 
     def hub_gather(cc, other):
@@ -357,17 +401,14 @@
         for i in range(parts):
             wait_recv(*chunk(x, 1 - h, i))
             forward(cc, x, 1 - h, i, r, edge)
-            if i % 2 == 0:
-                forward(cc, x, 1 - h, i, par, c)
+            forward(cc, x, 1 - h, i, par, c)
             wait_recv(*chunk(away, h, i))
-            if i % 2 == 1:
-                forward(cc, away, h, i, r, other)
             to_sib(cc, x, 1 - h, i)
             to_sib(cc, away, h, i)
-        for i in [*range(0, parts, 2), *range(1, parts, 2)]:
+        for i in range(direct, parts):
+            forward(cc, away, h, i, r, n_c - 1 - edge)
+        for i in range(parts):
             wait_recv(*chunk(away, 1 - h, i))
-            if i % 2 == 0:
-                forward(cc, away, 1 - h, i, r, edge)
             to_sib(cc, away, 1 - h, i)
 
     def edge_gather(cc, *_):
@@ -376,16 +417,20 @@
             wait_recv(*chunk(x, h, i))
             forward(cc, x, h, i, par, c)
             to_sib(cc, x, h, i)
-        for i in range(parts):
+        put_off(False)
+        off_copy().start()
+        for i in range(direct):
             wait_recv(*chunk(x, 1 - h, i))
-            if i % 2 == 1:
-                forward(cc, x, 1 - h, i, par, c)
+            forward(cc, x, 1 - h, i, par, c)
             to_sib(cc, x, 1 - h, i)
-            wait_recv(*chunk(away, h, i))
-            to_sib(cc, away, h, i)
-        for i in range(parts):
-            wait_recv(*chunk(away, 1 - h, i))
-            to_sib(cc, away, 1 - h, i)
+        order = [(away, h, i) for i in range(parts)]
+        for i in range(direct):
+            order += [(away, 1 - h, i + direct), (away, 1 - h, i)]
+        for i in range(direct, parts):
+            order.insert(len(order) - (parts - 1 - i), (x, 1 - h, i))
+        for s, g, i in order:
+            wait_recv(*chunk(s, g, i))
+            to_sib(cc, s, g, i)
 
     at_each_col(hub_gather, edge_gather)
     theirs = res.at[:, 1 - k]
@@ -394,7 +439,7 @@
     def _():
         pltpu.make_async_copy(mine, mine, s_mine.at[0]).wait()
 
-    off_copy.wait()
+    off_copy().wait()
     wait_sends(1)
 
     @pl.when(is_hub)
@@ -479,7 +524,7 @@
             f32(*linear.shape),
             f32(8 * packed + 8 * n_r * rows_dev * nb, LANES),
             dma(7 + n_c + 1),
-            dma(2 * n_c), dma(n_c + 1), dma(n_r), dma(1), dma(1), dma(1), dma(PARTS),
+            dma(3 * n_c), dma(n_c + 1), dma(n_r), dma(1), dma(1), dma(2), dma(PARTS),
             dma(2 * supers * PARTS), dma(1), dma(1), dma(4),
         ],
         compiler_params=pltpu.CompilerParams(
@@ -513,7 +558,7 @@
         and sigma_anc.shape[0] == sigma_anc.shape[1]
         and diag_inverse.shape[2] % LANES == 0
         and nb % 4 == 0
-        and rows_dev % SUBLANES == 0
+        and rows_dev % (2 * SUBLANES) == 0
         and width % (n_c * SUBLANES) == 0
         and len(pairs_of(nb)[0]) == len(pairs_of(nb)[1])
         and (len(pairs_of(nb)[0]) * LANES) % (2 * PARTS * SUBLANES) == 0

time: 43.8 us -> 41.4 us (0.945)
  Pallas kernels: 43 us -> 40.6 us
    pallas_call x1, Pallas kernels: 41.5 us -> 39.1 us  [fused_body(): pl.pallas_call(functools.partial(fused_kernel, n_r, n_c, supers, width, r...]
where the time goes in v6:
time: 41.4 us; the launch traced here: 41.2 us
  Pallas kernels  40.6 us (98%)
  between operations  0.64 us (2%)
    pallas_call x1, Pallas kernels, fused_body(): pl.pallas_call(functools.partial(fused_kernel, n_r, n_c, supers, width, r...  39.1 us
    pallas_call x1, Pallas kernels, fused_body(): pl.pallas_call(functools.partial(unpack_kernel, supers, nb), out_shape=(j...  1.52 us

profile of v6, /device:TPU:0, one launch (start us, length us, event | category | flops | bytes accessed | tf_op | source)
XLA Modules:
  0.0 41.2 jit_solution(17382032678571548520)
XLA Ops:
  0.6 39.1 %shard_map.59 = (f32[384,128]{1,0:T(8,128)S(1)}, f32[2,2,640,128]{3,2,1,0:T(8,128)S(1)}) custom-call(f32[192,192]{1,0:T(8,128)} %sig_hbm.1, f32[384,128]{1,0:T(8,128)} %bitcast.10, f32[2,512,128]{2,1,0:T(8,128)} %d_ref.1, s32[2,6]{1,0:T(2,128)} %pat_hbm.1), custom_call_target="tpu_custom_call" | custom-call | tf_op jit(solution)/shard_map/pallas_call | solution.py:499
  39.7 1.5 %shard_map.60 = (f32[384,128]{1,0:T(8,128)}, f32[2,512,512]{2,1,0:T(8,128)}) custom-call(f32[384,128]{1,0:T(8,128)S(1)} %get-tuple-element.6.off_in, f32[2,2,640,128]{3,2,1,0:T(8,128)S(1)} %get-tuple-element.7.res), custom_call_target="tpu_custom_call" | custom-call | tf_op jit(solution)/shard_map/pallas_call | solution.py:534

commit v7 on v6

--- a/solution.py
+++ b/solution.py
@@ -322,13 +322,14 @@
                         bulk[low + own_side][0] += math.prod(refs()[0].shape)
                     copy_to(*refs(), r, far, bulk_slot).start()
 
-    v_cols = lambda h: slice(h * LANES, (h + 1) * LANES)
+    v_cols = lambda h: slice(h * (width // 2), (h + 1) * (width // 2))
 
     @pl.when(is_hub)
     def _():
         sigma, ws = v_of(1)
-        for h in range(nb):
-            vpart[:, v_cols(h)] = vpart[:, v_cols(h)] + dot3(sigma, cut(ws, h))
+        for h in range(2):
+            wide = (ws[0][:, v_cols(h)], ws[1][:, v_cols(h)])
+            vpart[:, v_cols(h)] = vpart[:, v_cols(h)] + dot3(sigma, wide)
             copy_to(vpart.at[:, v_cols(h)], vrecv.at[:, v_cols(h)], s_v.at[0], sib, c, v_slot).start()
 
         wait_recv(scl.at[pl.ds(0, 2)], s_scl.at[0])
@@ -339,11 +340,13 @@
             @pl.when(k == core)
             def _():
                 ofs = {}
+                at = columns[core][0] * LANES
+                d_cols = jnp.concatenate([dfull[at:, lanes(j)] for j in columns[core]], axis=1)
+                v = dot3((vs[0][:, at:], vs[1][:, at:]), split(d_cols))
                 for slot, j in enumerate(columns[core]):
-                    at = j * LANES
-                    v = dot3((vs[0][:, at:], vs[1][:, at:]), split(dfull[at:, at : at + LANES]))
-                    of[slot] = v.reshape(n_r, 2, rows_dev, LANES)
-                    ofs[j] = split(v)
+                    part = v[:, lanes(slot)]
+                    of[slot] = part.reshape(n_r, 2, rows_dev, LANES)
+                    ofs[j] = split(part)
                 for row, col, kind in ((par, c, 1), (dia, c, 1), (r, mate, 0), (sib, mate, 0), (sib, c, 0), (par, mate, 1), (dia, mate, 1)):
                     post_hub(core, off_refs(row, c if col is c else mate, kind), row, col)
                 pltpu.make_async_copy(*off_refs(r, c, 0)()).start()

time: 41.4 us -> 41.4 us (level)
  no operation moved by 1% of the time
where the time goes in v7:
time: 41.4 us; the launch traced here: 41.2 us
  Pallas kernels  40.6 us (98%)
  between operations  0.64 us (2%)
    pallas_call x1, Pallas kernels, fused_body(): pl.pallas_call(functools.partial(fused_kernel, n_r, n_c, supers, width, r...  39.1 us
    pallas_call x1, Pallas kernels, fused_body(): pl.pallas_call(functools.partial(unpack_kernel, supers, nb), out_shape=(j...  1.52 us

profile of v7, /device:TPU:0, one launch (start us, length us, event | category | flops | bytes accessed | tf_op | source)
XLA Modules:
  0.0 41.2 jit_solution(14036668061431707409)
XLA Ops:
  0.6 39.1 %shard_map.59 = (f32[384,128]{1,0:T(8,128)S(1)}, f32[2,2,640,128]{3,2,1,0:T(8,128)S(1)}) custom-call(f32[192,192]{1,0:T(8,128)} %sig_hbm.1, f32[384,128]{1,0:T(8,128)} %bitcast.10, f32[2,512,128]{2,1,0:T(8,128)} %d_ref.1, s32[2,6]{1,0:T(2,128)} %pat_hbm.1), custom_call_target="tpu_custom_call" | custom-call | tf_op jit(solution)/shard_map/pallas_call | solution.py:502
  39.7 1.5 %shard_map.60 = (f32[384,128]{1,0:T(8,128)}, f32[2,512,512]{2,1,0:T(8,128)}) custom-call(f32[384,128]{1,0:T(8,128)S(1)} %get-tuple-element.6.off_in, f32[2,2,640,128]{3,2,1,0:T(8,128)S(1)} %get-tuple-element.7.res), custom_call_target="tpu_custom_call" | custom-call | tf_op jit(solution)/shard_map/pallas_call | solution.py:537
